TPU v7x, 256 devices: a whole 4x4x8 slice. The times are simulated.
256 devices in a mesh: samp: 4 (over x), gx: 8 (over y, core), gy: 8 (over z).
Axes of the slice: x: 4, y: 4, z: 8, core: 2. Of those that a mesh axis runs over, the one named last changes fastest.
Arguments:
- load: float32 [4, 2, 1024, 4096], P('samp', None, 'gx', 'gy'), parts along dimension 0, may hold values from -6 to 6
- material: int32 [4, 128, 512], P('samp', 'gx', 'gy'), parts along dimension 0, may hold values from 0 to 7
- lame_table: float32 [2, 8], replicated, may hold values from 0.3 to 6
Outputs:
- solution: float32 [4, 2, 1024, 4096], P('samp', None, 'gx', 'gy'), parts along dimension 0
- residual: float32 [4, 2, 1024, 4096], P('samp', None, 'gx', 'gy'), parts along dimension 0
There are 4 independent parts, one for each index of `samp`. A program takes and returns all parts, laid end to end along the dimension named above; an argument that names none is the same for every part. Nothing has to cross between parts.
All inputs are finite; a program needn't handle non-finite values.
Results may differ from a plain program's by a relative error of at most 0.0003.
Values sent between devices are 32-bit elements; how exact they have to be, the bound alone decides.
A program may use at most 64 MiB of HBM per device.

v0:
```python
import jax
import jax.numpy as jnp
from jax import lax
from jax.sharding import PartitionSpec as P

TILE = 8
CLASSES = 8
ITERS = 4


def shifted(block, axis, distance):
    devices = range(lax.axis_size(axis))
    route = [(i - distance, i) for i in devices if i - distance in devices]
    return lax.ppermute(block, axis, route)


def padded_2(array, sides, width):
    for axis, dim in sides:
        devices, length = (lax.axis_size(axis), array.shape[dim])
        up = [(i, (i + 1) % devices) for i in range(devices - 1)]
        down = [(j, i) for i, j in up]
        last = lax.slice_in_dim(array, length - width, length, axis=dim)
        leading = lax.slice_in_dim(array, 0, width, axis=dim)
        before = lax.ppermute(last, axis, up)
        after = lax.ppermute(leading, axis, down)
        array = jnp.concatenate([before, array, after], axis=dim)
    return array


def from_everyone(array, axis):
    devices = lax.axis_size(axis)
    return lax.all_to_all(
        jnp.broadcast_to(array[None], (devices, *array.shape)), axis, 0, 0, tiled=True
    )


def taken_together(array, axis):
    return from_everyone(array, axis).sum(axis=0)


def in_one(arrays, axis):
    ravelled, at, finished = (jnp.concatenate([a.reshape(-1) for a in arrays]), 0, [])
    running = taken_together(ravelled, axis)
    for a in arrays:
        finished.append(running[at : at + a.size].reshape(a.shape))
        at += a.size
    return tuple(finished)


def cell_moduli(material, lame_table):
    classes = jnp.arange(CLASSES, dtype=jnp.int32)
    match = (material[..., None] == classes).astype(jnp.float32)
    lam = jnp.sum(match * lame_table[0], axis=-1)
    mu = jnp.sum(match * lame_table[1], axis=-1)

    def expand(tiles):
        count, rows, cols = tiles.shape
        wide = jnp.broadcast_to(tiles[:, :, None, :, None], (count, rows, TILE, cols, TILE))
        return wide.reshape(count, rows * TILE, cols * TILE)

    return (expand(lam), expand(mu))


def cell_terms(nodes, lam, mu):
    low_low = nodes[..., :-1, :-1]
    high_low = nodes[..., 1:, :-1]
    low_high = nodes[..., :-1, 1:]
    high_high = nodes[..., 1:, 1:]
    along_x = 0.5 * (high_low + high_high - (low_low + low_high))
    along_y = 0.5 * (low_high + high_high - (low_low + high_low))
    strain_xx = along_x[:, 0]
    strain_yy = along_y[:, 1]
    shear = along_y[:, 0] + along_x[:, 1]
    stiff = lam + 2.0 * mu
    stress_xx = stiff * strain_xx + lam * strain_yy
    stress_yy = lam * strain_xx + stiff * strain_yy
    stress_xy = mu * shear
    plus = 0.5 * jnp.stack([stress_xx + stress_xy, stress_xy + stress_yy], axis=1)
    minus = 0.5 * jnp.stack([stress_xx - stress_xy, stress_xy - stress_yy], axis=1)
    return (plus, minus)


def on_device(load, material, lame_table):
    rows = load.shape[2]
    cols = load.shape[3]
    lam, mu = cell_moduli(material, lame_table)
    moduli = jnp.stack([lam, mu], axis=1)
    row_before = shifted(moduli[:, :, rows - 1 :, :], "gx", 1)
    widened = jnp.concatenate([row_before, moduli], axis=2)
    col_before = shifted(widened[:, :, :, cols - 1 :], "gy", 1)
    widened = jnp.concatenate([col_before, widened], axis=3)
    lam_rim = widened[:, 0]
    mu_rim = widened[:, 1]

    def operate(field):
        padded = padded_2(field, (("gx", 2), ("gy", 3)), 1)
        plus, minus = cell_terms(padded, lam_rim, mu_rim)
        forces = plus[..., :-1, :-1] - plus[..., 1:, 1:] + minus[..., :-1, 1:] - minus[..., 1:, :-1]
        return 0.05 * field + forces

    solution = jnp.zeros_like(load)
    residual = load
    w_vec = operate(residual)
    z_vec = jnp.zeros_like(load)
    q_vec = jnp.zeros_like(load)
    p_vec = jnp.zeros_like(load)
    gamma_prev = jnp.ones((load.shape[0],), jnp.float32)
    alpha_prev = jnp.ones((load.shape[0],), jnp.float32)
    for step in range(ITERS):
        local_gamma = jnp.sum(residual * residual, axis=(1, 2, 3))
        local_delta = jnp.sum(w_vec * residual, axis=(1, 2, 3))
        gamma, delta = in_one((local_gamma, local_delta), ("gx", "gy"))
        if step + 1 < ITERS:
            n_vec = operate(w_vec)
        if step == 0:
            beta = jnp.zeros_like(gamma)
            alpha = gamma / delta
        else:
            beta = gamma / gamma_prev
            alpha = gamma / (delta - beta * gamma / alpha_prev)
        beta_b = beta[:, None, None, None]
        alpha_b = alpha[:, None, None, None]
        if step + 1 < ITERS:
            z_vec = n_vec + beta_b * z_vec
        q_vec = w_vec + beta_b * q_vec
        p_vec = residual + beta_b * p_vec
        solution = solution + alpha_b * p_vec
        residual = residual - alpha_b * q_vec
        if step + 1 < ITERS:
            w_vec = w_vec - alpha_b * z_vec
        gamma_prev = gamma
        alpha_prev = alpha
    return (solution, residual)


def solution(mesh):
    return jax.shard_map(
        on_device,
        mesh=mesh,
        in_specs=(P("samp", None, "gx", "gy"), P("samp", "gx", "gy"), P()),
        out_specs=(P("samp", None, "gx", "gy"), P("samp", None, "gx", "gy")),
        check_vma=False,
    )
```

profile of v0, /device:TPU:1, one launch (start us, length us, event | category | flops | bytes accessed | tf_op | source)
XLA Modules:
  0.0 176.2 jit_solution(7045586676902684753)
XLA Ops:
  0.6 0.8 slice_bitcast_fusion.1
  1.4 0.8 select_reduce_fusion
  2.2 2.5 %broadcast_in_dim.18 = f32[16,8,64,8]{3,2,1,0:T(8,128)} broadcast(f32[16,64]{1,0:T(8,128)S(1)} %get-tuple-element.10), dimensions={0,2} | broadcast | bytes 266240 | tf_op jit(solution)/shard_map/broadcast_in_dim | solution.py:58
  4.7 4.0 %broadcast_in_dim.19 = f32[1,1,128,512]{3,2,1,0:T(8,128)S(1)} reshape(f32[16,8,64,8]{3,2,1,0:T(8,128)} %broadcast_in_dim.18) | data formatting | bytes 524288 | tf_op jit(solution)/shard_map/broadcast_in_dim | solution.py:58
  8.7 2.5 %broadcast_in_dim.16 = f32[16,8,64,8]{3,2,1,0:T(8,128)} broadcast(f32[16,64]{1,0:T(8,128)S(1)} %get-tuple-element.11), dimensions={0,2} | broadcast | bytes 266240 | tf_op jit(solution)/shard_map/broadcast_in_dim | solution.py:58
  11.3 4.0 %broadcast_in_dim.17 = f32[1,1,128,512]{3,2,1,0:T(8,128)S(1)} reshape(f32[16,8,64,8]{3,2,1,0:T(8,128)} %broadcast_in_dim.16) | data formatting | bytes 524288 | tf_op jit(solution)/shard_map/broadcast_in_dim | solution.py:58
  15.3 4.6 %collective-permute-start = (f32[1,2,1,512]{3,2,1,0:T(1,128)S(1)}, f32[1,2,1,512]{3,2,1,0:T(1,128)S(1)}, u32[]{:S(2)}, u32[]{:S(2)}) collective-permute-start(f32[1,2,1,512]{3,2,1,0:T(1,128)S(1)} %slice.328), channel_id=1, source_target_pairs={{0,8},{8,16},{16,24},{24,32},{32,40},{40,48},{48,56},{1,9},{9,17},... | collective-permute-start | bytes 12296 | tf_op jit(solution)/shard_map/ppermute | solution.py:14
  20.0 1.9 %collective-permute-start.2 = (f32[1,2,1,512]{3,2,1,0:T(1,128)S(1)}, f32[1,2,1,512]{3,2,1,0:T(1,128)S(1)}, u32[]{:S(2)}, u32[]{:S(2)}) collective-permute-start(f32[1,2,1,512]{3,2,1,0:T(1,128)S(1)} %get-tuple-element.74), channel_id=1, source_target_pairs={{0,8},{8,16},{16,24},{24,32},{32,40},{40,48},{48,56},{1,9},{9,17},... | collective-permute-start | bytes 12296 | tf_op jit(solution)/shard_map/ppermute | solution.py:24
  21.9 2.4 %collective-permute-start.3 = (f32[1,2,1,512]{3,2,1,0:T(1,128)S(1)}, f32[1,2,1,512]{3,2,1,0:T(1,128)S(1)}, u32[]{:S(2)}, u32[]{:S(2)}) collective-permute-start(f32[1,2,1,512]{3,2,1,0:T(1,128)S(1)} %get-tuple-element.75), channel_id=1, source_target_pairs={{8,0},{16,8},{24,16},{32,24},{40,32},{48,40},{56,48},{9,1},{17,9},... | collective-permute-start | bytes 12296 | tf_op jit(solution)/shard_map/ppermute | solution.py:25
  24.4 3.5 %collective-permute-start.1 = (f32[1,2,129,1]{3,2,1,0:T(8,128)S(1)}, f32[1,2,129,1]{3,2,1,0:T(8,128)S(1)}, u32[]{:S(2)}, u32[]{:S(2)}) collective-permute-start(f32[1,2,129,1]{3,2,1,0:T(8,128)S(1)} %pad_maximum_fusion.16), channel_id=1, source_target_pairs={{0,1},{1,2},{2,3},{3,4},{4,5},{5,6},{6,7},{8,9},{9,10},{10,11},{11... | collective-permute-start | bytes 3104 | tf_op jit(solution)/shard_map/ppermute | solution.py:14
  28.1 3.5 %collective-permute-start.4 = (f32[1,2,130,1]{3,2,1,0:T(8,128)S(1)}, f32[1,2,130,1]{3,2,1,0:T(8,128)S(1)}, u32[]{:S(2)}, u32[]{:S(2)}) collective-permute-start(f32[1,2,130,1]{3,2,1,0:T(8,128)S(1)} %get-tuple-element.66), channel_id=1, source_target_pairs={{0,1},{1,2},{2,3},{3,4},{4,5},{5,6},{6,7},{8,9},{9,10},{10,11},{11... | collective-permute-start | bytes 3128 | tf_op jit(solution)/shard_map/ppermute | solution.py:24
  31.7 1.3 collective-permute-start.5
  33.0 0.3 maximum_maximum_fusion
  33.3 1.8 collective-permute-done.4
  35.0 4.2 %collective-permute-done.5 = f32[1,2,130,1]{3,2,1,0:T(8,128)S(1)} collective-permute-done((f32[1,2,130,1]{3,2,1,0:T(8,128)S(1)}, f32[1,2,130,1]{3,2,1,0:T(8,128)S(1)}, u32[]{:S(2)}, u32[]{:S(2)}) %collective-permute-start.5) | collective-permute-done | bytes 1072 | tf_op jit(solution)/shard_map/ppermute | solution.py:25
  39.2 0.3 maximum_maximum_fusion.1
  39.5 0.3 subtract_multiply_fusion.7
  39.9 0.2 fusion.27
  40.3 1.0 multiply_reduce_fusion.7
  41.3 3.7 %collective-permute-start.6 = (f32[1,2,1,512]{3,2,1,0:T(1,128)S(1)}, f32[1,2,1,512]{3,2,1,0:T(1,128)S(1)}, u32[]{:S(2)}, u32[]{:S(2)}) collective-permute-start(f32[1,2,1,512]{3,2,1,0:T(1,128)S(1)} %get-tuple-element.72), channel_id=1, source_target_pairs={{0,8},{8,16},{16,24},{24,32},{32,40},{40,48},{48,56},{1,9},{9,17},... | collective-permute-start | bytes 12296 | tf_op jit(solution)/shard_map/ppermute | solution.py:24
  45.0 1.9 %collective-permute-start.7 = (f32[1,2,1,512]{3,2,1,0:T(1,128)S(1)}, f32[1,2,1,512]{3,2,1,0:T(1,128)S(1)}, u32[]{:S(2)}, u32[]{:S(2)}) collective-permute-start(f32[1,2,1,512]{3,2,1,0:T(1,128)S(1)} %get-tuple-element.73), channel_id=1, source_target_pairs={{8,0},{16,8},{24,16},{32,24},{40,32},{48,40},{56,48},{9,1},{17,9},... | collective-permute-start | bytes 12296 | tf_op jit(solution)/shard_map/ppermute | solution.py:25
  46.9 1.4 pad_maximum_fusion.17
  48.3 19.7 %all_to_all.24 = f32[64,1,2]{2,1,0:T(1,128)S(1)} all-to-all(f32[64,1,2]{2,1,0:T(1,128)S(1)} %broadcast_in_dim.20), channel_id=1, replica_groups=mesh['samp'=4,'gx'=8,'gy'=8] {'gx','gy'}, dimensions={0} | all-to-all | bytes 1024 | tf_op jit(solution)/shard_map/all_to_all | solution.py:32
  68.3 2.3 %collective-permute-start.8 = (f32[1,2,130,1]{3,2,1,0:T(8,128)S(1)}, f32[1,2,130,1]{3,2,1,0:T(8,128)S(1)}, u32[]{:S(2)}, u32[]{:S(2)}) collective-permute-start(f32[1,2,130,1]{3,2,1,0:T(8,128)S(1)} %get-tuple-element.62), channel_id=1, source_target_pairs={{0,1},{1,2},{2,3},{3,4},{4,5},{5,6},{6,7},{8,9},{9,10},{10,11},{11... | collective-permute-start | bytes 3128 | tf_op jit(solution)/shard_map/ppermute | solution.py:24
  70.5 1.3 collective-permute-start.9
  71.8 0.6 fusion.35
  73.7 2.6 %collective-permute-done.9 = f32[1,2,130,1]{3,2,1,0:T(8,128)S(1)} collective-permute-done((f32[1,2,130,1]{3,2,1,0:T(8,128)S(1)}, f32[1,2,130,1]{3,2,1,0:T(8,128)S(1)}, u32[]{:S(2)}, u32[]{:S(2)}) %collective-permute-start.9) | collective-permute-done | bytes 1072 | tf_op jit(solution)/shard_map/ppermute | solution.py:25
  76.3 0.3 maximum_maximum_fusion.2
  76.6 0.3 subtract_multiply_fusion.5
  76.9 0.2 fusion.21
  77.1 0.2 fusion.23
  77.4 2.2 %multiply_reduce_fusion.5 = (f32[]{:T(128)}, f32[]{:T(128)}, f32[1,2,128,512]{3,2,1,0:T(8,128)S(1)}, f32[1,2,128,512]{3,2,1,0:T(8,128)}, f32[1,2,128,512]{3,2,1,0:T(8,128)}) fusion(f32[1,2,128,512]{3,2,1,0:T(8,128)S(1)} %get-tuple-element.35, f32[]{:T(128)} %bitcast.5, f32[1,2,129,513]{3,2,1,0:T(8,128)S(1)} %maximum_multiply_fusion.3, ...), kind=kLoop, calls=%fused_computation.58 | loop fusion | flops 1703934 | bytes 4718604 | tf_op jit(solution)/shard_map/reduce_sum | solution.py:110
  79.6 4.4 %collective-permute-start.10 = (f32[1,2,1,512]{3,2,1,0:T(1,128)S(1)}, f32[1,2,1,512]{3,2,1,0:T(1,128)S(1)}, u32[]{:S(2)}, u32[]{:S(2)}) collective-permute-start(f32[1,2,1,512]{3,2,1,0:T(1,128)S(1)} %get-tuple-element.70), channel_id=1, source_target_pairs={{0,8},{8,16},{16,24},{24,32},{32,40},{40,48},{48,56},{1,9},{9,17},... | collective-permute-start | bytes 12296 | tf_op jit(solution)/shard_map/ppermute | solution.py:24
  84.0 1.9 %collective-permute-start.11 = (f32[1,2,1,512]{3,2,1,0:T(1,128)S(1)}, f32[1,2,1,512]{3,2,1,0:T(1,128)S(1)}, u32[]{:S(2)}, u32[]{:S(2)}) collective-permute-start(f32[1,2,1,512]{3,2,1,0:T(1,128)S(1)} %get-tuple-element.71), channel_id=1, source_target_pairs={{8,0},{16,8},{24,16},{32,24},{40,32},{48,40},{56,48},{9,1},{17,9},... | collective-permute-start | bytes 12296 | tf_op jit(solution)/shard_map/ppermute | solution.py:25
  85.9 1.3 pad_maximum_fusion.18
  87.3 15.0 %all_to_all.25 = f32[64,1,2]{2,1,0:T(1,128)S(1)} all-to-all(f32[64,1,2]{2,1,0:T(1,128)S(1)} %broadcast_in_dim.21), channel_id=1, replica_groups=mesh['samp'=4,'gx'=8,'gy'=8] {'gx','gy'}, dimensions={0} | all-to-all | bytes 1024 | tf_op jit(solution)/shard_map/all_to_all | solution.py:32
  102.4 2.3 %collective-permute-start.12 = (f32[1,2,130,1]{3,2,1,0:T(8,128)S(1)}, f32[1,2,130,1]{3,2,1,0:T(8,128)S(1)}, u32[]{:S(2)}, u32[]{:S(2)}) collective-permute-start(f32[1,2,130,1]{3,2,1,0:T(8,128)S(1)} %get-tuple-element.58), channel_id=1, source_target_pairs={{0,1},{1,2},{2,3},{3,4},{4,5},{5,6},{6,7},{8,9},{9,10},{10,11},{11... | collective-permute-start | bytes 3128 | tf_op jit(solution)/shard_map/ppermute | solution.py:24
  104.7 1.3 collective-permute-start.13
  106.0 0.6 fusion.34
  111.0 0.3 maximum_maximum_fusion.3
  111.3 0.3 subtract_multiply_fusion.3
  111.6 0.2 fusion.17
  111.8 0.2 fusion.19
  112.1 0.7 copy-done.1
  112.8 0.2 copy-done.5
  113.0 2.2 %multiply_reduce_fusion.3 = (f32[]{:T(128)}, f32[]{:T(128)}, f32[1,2,128,512]{3,2,1,0:T(8,128)S(1)}, f32[1,2,128,512]{3,2,1,0:T(8,128)}, f32[1,2,128,512]{3,2,1,0:T(8,128)}) fusion(f32[1,2,128,512]{3,2,1,0:T(8,128)S(1)} %get-tuple-element.27, f32[]{:T(128)} %bitcast.8, f32[1,2,128,512]{3,2,1,0:T(8,128)S(1)} %copy-done.5, f32[]{:T(128)} %bitcast.9, ...), kind=kLoop, calls=%fused_computation.53 | loop fusion | flops 2228222 | bytes 5767184 | tf_op jit(solution)/shard_map/reduce_sum | solution.py:110
  115.2 3.9 %collective-permute-start.14 = (f32[1,2,1,512]{3,2,1,0:T(1,128)S(1)}, f32[1,2,1,512]{3,2,1,0:T(1,128)S(1)}, u32[]{:S(2)}, u32[]{:S(2)}) collective-permute-start(f32[1,2,1,512]{3,2,1,0:T(1,128)S(1)} %get-tuple-element.68), channel_id=1, source_target_pairs={{0,8},{8,16},{16,24},{24,32},{32,40},{40,48},{48,56},{1,9},{9,17},... | collective-permute-start | bytes 12296 | tf_op jit(solution)/shard_map/ppermute | solution.py:24
  119.1 1.9 %collective-permute-start.15 = (f32[1,2,1,512]{3,2,1,0:T(1,128)S(1)}, f32[1,2,1,512]{3,2,1,0:T(1,128)S(1)}, u32[]{:S(2)}, u32[]{:S(2)}) collective-permute-start(f32[1,2,1,512]{3,2,1,0:T(1,128)S(1)} %get-tuple-element.69), channel_id=1, source_target_pairs={{8,0},{16,8},{24,16},{32,24},{40,32},{48,40},{56,48},{9,1},{17,9},... | collective-permute-start | bytes 12296 | tf_op jit(solution)/shard_map/ppermute | solution.py:25
  121.0 1.3 pad_maximum_fusion.19
  122.4 16.3 %all_to_all.26 = f32[64,1,2]{2,1,0:T(1,128)S(1)} all-to-all(f32[64,1,2]{2,1,0:T(1,128)S(1)} %broadcast_in_dim.22), channel_id=1, replica_groups=mesh['samp'=4,'gx'=8,'gy'=8] {'gx','gy'}, dimensions={0} | all-to-all | bytes 1024 | tf_op jit(solution)/shard_map/all_to_all | solution.py:32
  138.9 2.3 %collective-permute-start.16 = (f32[1,2,130,1]{3,2,1,0:T(8,128)S(1)}, f32[1,2,130,1]{3,2,1,0:T(8,128)S(1)}, u32[]{:S(2)}, u32[]{:S(2)}) collective-permute-start(f32[1,2,130,1]{3,2,1,0:T(8,128)S(1)} %get-tuple-element.54), channel_id=1, source_target_pairs={{0,1},{1,2},{2,3},{3,4},{4,5},{5,6},{6,7},{8,9},{9,10},{10,11},{11... | collective-permute-start | bytes 3128 | tf_op jit(solution)/shard_map/ppermute | solution.py:24
  141.2 1.3 collective-permute-start.17
  142.5 0.6 fusion.33
  147.1 0.3 maximum_maximum_fusion.4
  147.4 0.3 subtract_multiply_fusion.1
  147.6 0.2 fusion.13
  147.8 0.2 fusion.15
  148.2 0.7 copy-done.3
  148.8 0.2 copy-done.4
  149.0 2.2 %multiply_reduce_fusion.1 = (f32[]{:T(128)}, f32[]{:T(128)}, f32[1,2,128,512]{3,2,1,0:T(8,128)}, f32[1,2,128,512]{3,2,1,0:T(8,128)}) fusion(f32[1,2,128,512]{3,2,1,0:T(8,128)S(1)} %copy-done.3, f32[]{:T(128)} %bitcast.12, f32[1,2,128,512]{3,2,1,0:T(8,128)S(1)} %get-tuple-element.19, f32[1,2,128,512]{3,2,1,0:T(8,128)S(1)} %copy-done.4, f32[]{:T(128)} %bitcast.13, ...), kind=kLoop, calls=%fused_computation.48 | loop fusion | flops 2490366 | bytes 5767188 | tf_op jit(solution)/shard_map/reduce_sum | solution.py:110
  151.2 1.3 pad_maximum_fusion.20
  152.6 16.4 %all_to_all.27 = f32[64,1,2]{2,1,0:T(1,128)S(1)} all-to-all(f32[64,1,2]{2,1,0:T(1,128)S(1)} %broadcast_in_dim.23), channel_id=1, replica_groups=mesh['samp'=4,'gx'=8,'gy'=8] {'gx','gy'}, dimensions={0} | all-to-all | bytes 1024 | tf_op jit(solution)/shard_map/all_to_all | solution.py:32
  169.1 0.6 fusion.32
  173.6 2.7 %multiply_subtract_fusion = (f32[1,2,128,512]{3,2,1,0:T(8,128)}, f32[1,2,128,512]{3,2,1,0:T(8,128)}) fusion(f32[1,2,128,512]{3,2,1,0:T(8,128)} %get-tuple-element.12, f32[1,2,128,512]{3,2,1,0:T(8,128)} %get-tuple-element.13, f32[]{:T(128)} %bitcast.17, f32[]{:T(128)} %bitcast.16, f32[1,2,128,512]{3,2,1,0:T(8,128)} %get-tuple-element.21, f32[]{:T(128)} %bitcast.12, ...), kind=kLoop, calls=%fused_computation.45 | loop fusion | flops 2490368 | bytes 3670044 | tf_op jit(solution)/shard_map/sub | solution.py:128
  (55 shorter events, 1.9 us)
Async XLA Ops:
  8.7 11.2 %copy-start = (f32[1,2,128,512]{3,2,1,0:T(8,128)S(1)}, f32[1,2,128,512]{3,2,1,0:T(8,128)}, u32[]{:S(2)}) copy-start(f32[1,2,128,512]{3,2,1,0:T(8,128)} %param.3) | copy-start | bytes 1572868
  15.3 9.0 %collective-permute-start = (f32[1,2,1,512]{3,2,1,0:T(1,128)S(1)}, f32[1,2,1,512]{3,2,1,0:T(1,128)S(1)}, u32[]{:S(2)}, u32[]{:S(2)}) collective-permute-start(f32[1,2,1,512]{3,2,1,0:T(1,128)S(1)} %slice.328), channel_id=1, source_target_pairs={{0,8},{8,16},{16,24},{24,32},{32,40},{40,48},{48,56},{1,9},{9,17},... | collective-permute-start | bytes 12296 | tf_op jit(solution)/shard_map/ppermute | solution.py:14
  20.0 8.0 %collective-permute-start.2 = (f32[1,2,1,512]{3,2,1,0:T(1,128)S(1)}, f32[1,2,1,512]{3,2,1,0:T(1,128)S(1)}, u32[]{:S(2)}, u32[]{:S(2)}) collective-permute-start(f32[1,2,1,512]{3,2,1,0:T(1,128)S(1)} %get-tuple-element.74), channel_id=1, source_target_pairs={{0,8},{8,16},{16,24},{24,32},{32,40},{40,48},{48,56},{1,9},{9,17},... | collective-permute-start | bytes 12296 | tf_op jit(solution)/shard_map/ppermute | solution.py:24
  21.9 6.1 %collective-permute-start.3 = (f32[1,2,1,512]{3,2,1,0:T(1,128)S(1)}, f32[1,2,1,512]{3,2,1,0:T(1,128)S(1)}, u32[]{:S(2)}, u32[]{:S(2)}) collective-permute-start(f32[1,2,1,512]{3,2,1,0:T(1,128)S(1)} %get-tuple-element.75), channel_id=1, source_target_pairs={{8,0},{16,8},{24,16},{32,24},{40,32},{48,40},{56,48},{9,1},{17,9},... | collective-permute-start | bytes 12296 | tf_op jit(solution)/shard_map/ppermute | solution.py:25
  24.4 8.6 %collective-permute-start.1 = (f32[1,2,129,1]{3,2,1,0:T(8,128)S(1)}, f32[1,2,129,1]{3,2,1,0:T(8,128)S(1)}, u32[]{:S(2)}, u32[]{:S(2)}) collective-permute-start(f32[1,2,129,1]{3,2,1,0:T(8,128)S(1)} %pad_maximum_fusion.16), channel_id=1, source_target_pairs={{0,1},{1,2},{2,3},{3,4},{4,5},{5,6},{6,7},{8,9},{9,10},{10,11},{11... | collective-permute-start | bytes 3104 | tf_op jit(solution)/shard_map/ppermute | solution.py:14
  28.1 6.9 %collective-permute-start.4 = (f32[1,2,130,1]{3,2,1,0:T(8,128)S(1)}, f32[1,2,130,1]{3,2,1,0:T(8,128)S(1)}, u32[]{:S(2)}, u32[]{:S(2)}) collective-permute-start(f32[1,2,130,1]{3,2,1,0:T(8,128)S(1)} %get-tuple-element.66), channel_id=1, source_target_pairs={{0,1},{1,2},{2,3},{3,4},{4,5},{5,6},{6,7},{8,9},{9,10},{10,11},{11... | collective-permute-start | bytes 3128 | tf_op jit(solution)/shard_map/ppermute | solution.py:24
  31.7 7.5 %collective-permute-start.5 = (f32[1,2,130,1]{3,2,1,0:T(8,128)S(1)}, f32[1,2,130,1]{3,2,1,0:T(8,128)S(1)}, u32[]{:S(2)}, u32[]{:S(2)}) collective-permute-start(f32[1,2,130,1]{3,2,1,0:T(8,128)S(1)} %get-tuple-element.67), channel_id=1, source_target_pairs={{1,0},{2,1},{3,2},{4,3},{5,4},{6,5},{7,6},{9,8},{10,9},{11,10},{12... | collective-permute-start | bytes 3128 | tf_op jit(solution)/shard_map/ppermute | solution.py:25
  41.3 26.8 %collective-permute-start.6 = (f32[1,2,1,512]{3,2,1,0:T(1,128)S(1)}, f32[1,2,1,512]{3,2,1,0:T(1,128)S(1)}, u32[]{:S(2)}, u32[]{:S(2)}) collective-permute-start(f32[1,2,1,512]{3,2,1,0:T(1,128)S(1)} %get-tuple-element.72), channel_id=1, source_target_pairs={{0,8},{8,16},{16,24},{24,32},{32,40},{40,48},{48,56},{1,9},{9,17},... | collective-permute-start | bytes 12296 | tf_op jit(solution)/shard_map/ppermute | solution.py:24
  45.0 23.1 %collective-permute-start.7 = (f32[1,2,1,512]{3,2,1,0:T(1,128)S(1)}, f32[1,2,1,512]{3,2,1,0:T(1,128)S(1)}, u32[]{:S(2)}, u32[]{:S(2)}) collective-permute-start(f32[1,2,1,512]{3,2,1,0:T(1,128)S(1)} %get-tuple-element.73), channel_id=1, source_target_pairs={{8,0},{16,8},{24,16},{32,24},{40,32},{48,40},{56,48},{9,1},{17,9},... | collective-permute-start | bytes 12296 | tf_op jit(solution)/shard_map/ppermute | solution.py:25
  68.3 5.5 %collective-permute-start.8 = (f32[1,2,130,1]{3,2,1,0:T(8,128)S(1)}, f32[1,2,130,1]{3,2,1,0:T(8,128)S(1)}, u32[]{:S(2)}, u32[]{:S(2)}) collective-permute-start(f32[1,2,130,1]{3,2,1,0:T(8,128)S(1)} %get-tuple-element.62), channel_id=1, source_target_pairs={{0,1},{1,2},{2,3},{3,4},{4,5},{5,6},{6,7},{8,9},{9,10},{10,11},{11... | collective-permute-start | bytes 3128 | tf_op jit(solution)/shard_map/ppermute | solution.py:24
  70.5 5.8 %collective-permute-start.9 = (f32[1,2,130,1]{3,2,1,0:T(8,128)S(1)}, f32[1,2,130,1]{3,2,1,0:T(8,128)S(1)}, u32[]{:S(2)}, u32[]{:S(2)}) collective-permute-start(f32[1,2,130,1]{3,2,1,0:T(8,128)S(1)} %get-tuple-element.63), channel_id=1, source_target_pairs={{1,0},{2,1},{3,2},{4,3},{5,4},{6,5},{7,6},{9,8},{10,9},{11,10},{12... | collective-permute-start | bytes 3128 | tf_op jit(solution)/shard_map/ppermute | solution.py:25
  79.6 22.7 %collective-permute-start.10 = (f32[1,2,1,512]{3,2,1,0:T(1,128)S(1)}, f32[1,2,1,512]{3,2,1,0:T(1,128)S(1)}, u32[]{:S(2)}, u32[]{:S(2)}) collective-permute-start(f32[1,2,1,512]{3,2,1,0:T(1,128)S(1)} %get-tuple-element.70), channel_id=1, source_target_pairs={{0,8},{8,16},{16,24},{24,32},{32,40},{40,48},{48,56},{1,9},{9,17},... | collective-permute-start | bytes 12296 | tf_op jit(solution)/shard_map/ppermute | solution.py:24
  84.0 18.3 %collective-permute-start.11 = (f32[1,2,1,512]{3,2,1,0:T(1,128)S(1)}, f32[1,2,1,512]{3,2,1,0:T(1,128)S(1)}, u32[]{:S(2)}, u32[]{:S(2)}) collective-permute-start(f32[1,2,1,512]{3,2,1,0:T(1,128)S(1)} %get-tuple-element.71), channel_id=1, source_target_pairs={{8,0},{16,8},{24,16},{32,24},{40,32},{48,40},{56,48},{9,1},{17,9},... | collective-permute-start | bytes 12296 | tf_op jit(solution)/shard_map/ppermute | solution.py:25
  102.4 8.5 %collective-permute-start.12 = (f32[1,2,130,1]{3,2,1,0:T(8,128)S(1)}, f32[1,2,130,1]{3,2,1,0:T(8,128)S(1)}, u32[]{:S(2)}, u32[]{:S(2)}) collective-permute-start(f32[1,2,130,1]{3,2,1,0:T(8,128)S(1)} %get-tuple-element.58), channel_id=1, source_target_pairs={{0,1},{1,2},{2,3},{3,4},{4,5},{5,6},{6,7},{8,9},{9,10},{10,11},{11... | collective-permute-start | bytes 3128 | tf_op jit(solution)/shard_map/ppermute | solution.py:24
  104.7 6.3 %collective-permute-start.13 = (f32[1,2,130,1]{3,2,1,0:T(8,128)S(1)}, f32[1,2,130,1]{3,2,1,0:T(8,128)S(1)}, u32[]{:S(2)}, u32[]{:S(2)}) collective-permute-start(f32[1,2,130,1]{3,2,1,0:T(8,128)S(1)} %get-tuple-element.59), channel_id=1, source_target_pairs={{1,0},{2,1},{3,2},{4,3},{5,4},{6,5},{7,6},{9,8},{10,9},{11,10},{12... | collective-permute-start | bytes 3128 | tf_op jit(solution)/shard_map/ppermute | solution.py:25
  111.8 1.0 copy-start.1
  111.8 1.2 copy-start.5
  115.2 23.6 %collective-permute-start.14 = (f32[1,2,1,512]{3,2,1,0:T(1,128)S(1)}, f32[1,2,1,512]{3,2,1,0:T(1,128)S(1)}, u32[]{:S(2)}, u32[]{:S(2)}) collective-permute-start(f32[1,2,1,512]{3,2,1,0:T(1,128)S(1)} %get-tuple-element.68), channel_id=1, source_target_pairs={{0,8},{8,16},{16,24},{24,32},{32,40},{40,48},{48,56},{1,9},{9,17},... | collective-permute-start | bytes 12296 | tf_op jit(solution)/shard_map/ppermute | solution.py:24
  119.1 19.7 %collective-permute-start.15 = (f32[1,2,1,512]{3,2,1,0:T(1,128)S(1)}, f32[1,2,1,512]{3,2,1,0:T(1,128)S(1)}, u32[]{:S(2)}, u32[]{:S(2)}) collective-permute-start(f32[1,2,1,512]{3,2,1,0:T(1,128)S(1)} %get-tuple-element.69), channel_id=1, source_target_pairs={{8,0},{16,8},{24,16},{32,24},{40,32},{48,40},{56,48},{9,1},{17,9},... | collective-permute-start | bytes 12296 | tf_op jit(solution)/shard_map/ppermute | solution.py:25
  138.9 8.1 %collective-permute-start.16 = (f32[1,2,130,1]{3,2,1,0:T(8,128)S(1)}, f32[1,2,130,1]{3,2,1,0:T(8,128)S(1)}, u32[]{:S(2)}, u32[]{:S(2)}) collective-permute-start(f32[1,2,130,1]{3,2,1,0:T(8,128)S(1)} %get-tuple-element.54), channel_id=1, source_target_pairs={{0,1},{1,2},{2,3},{3,4},{4,5},{5,6},{6,7},{8,9},{9,10},{10,11},{11... | collective-permute-start | bytes 3128 | tf_op jit(solution)/shard_map/ppermute | solution.py:24
  141.2 5.9 %collective-permute-start.17 = (f32[1,2,130,1]{3,2,1,0:T(8,128)S(1)}, f32[1,2,130,1]{3,2,1,0:T(8,128)S(1)}, u32[]{:S(2)}, u32[]{:S(2)}) collective-permute-start(f32[1,2,130,1]{3,2,1,0:T(8,128)S(1)} %get-tuple-element.55), channel_id=1, source_target_pairs={{1,0},{2,1},{3,2},{4,3},{5,4},{6,5},{7,6},{9,8},{10,9},{11,10},{12... | collective-permute-start | bytes 3128 | tf_op jit(solution)/shard_map/ppermute | solution.py:25
  147.8 1.0 copy-start.3
  147.8 1.2 copy-start.4
  148.0 25.6 %copy-start.2 = (f32[1,2,128,512]{3,2,1,0:T(8,128)S(1)}, f32[1,2,128,512]{3,2,1,0:T(8,128)}, u32[]{:S(2)}) copy-start(f32[1,2,128,512]{3,2,1,0:T(8,128)} %get-tuple-element.29) | copy-start | bytes 1572868
where the time goes:
time: 177 us; the launch traced here: 176 us
  blocking collectives  67.4 us (38%)
  starting transfers between devices  45.8 us (26%)
  other arithmetic  21.8 us (12%)
  local copies, waits for them, and re-layouts  18.1 us (10%)
  between operations  14.6 us (8%)
  waiting for transfers between devices  8.58 us (5%)
    all_to_all x4, blocking collectives, from_everyone(): lax.all_to_all(jnp.broadcast_to(array[None], (devices, *array.shape)), ax...  67.4 us
    ppermute x8, starting transfers between devices, padded_2(): before = lax.ppermute(last, axis, up)  24.3 us
    ppermute x8, starting transfers between devices, padded_2(): after = lax.ppermute(leading, axis, down)  13.3 us
    broadcast_in_dim x4, local copies, waits for them, and re-layouts, expand(): jnp.broadcast_to(tiles[:, :, None, :, None], (count, rows, TILE, cols, TI...  13 us
    ppermute x2, starting transfers between devices, shifted(): return lax.ppermute(block, axis, route)  8.13 us
    reduce_sum x4, other arithmetic, on_device(): local_gamma = jnp.sum(residual * residual, axis=(1, 2, 3))  7.56 us
    ppermute x8, waiting for transfers between devices, padded_2(): after = lax.ppermute(leading, axis, down)  6.8 us
    concatenate x4, other arithmetic, in_one(): jnp.concatenate([a.reshape(-1) for a in arrays])  5.32 us
  transfers between devices with their start and end apart: 18, of which 3 were waited for; matrix products, arithmetic and copies ran while one was open for 4% of the time, Pallas kernels for 0%

commit v1 on v0

v1 whole, which is shorter than its diff:
```python
import functools

import jax
import jax.numpy as jnp
from jax import lax
from jax.experimental import pallas as pl
from jax.experimental.pallas import tpu as pltpu
from jax.sharding import PartitionSpec as P

TILE = 8
CLASSES = 8
ITERS = 4
LEVELS = ITERS
MASS = 0.05
SPREAD = 1.5
CENTRE = 1.5
DIAG = -CENTRE / SPREAD
MESH = pl.DeviceIdType.MESH
WAYS = [(dx, dy) for dx in (-1, 0, 1) for dy in (-1, 0, 1) if (dx, dy) != (0, 0)]
SIDE = 5
DIAGONAL = [w for w in WAYS if w[0] and w[1]]


def loop(count, body, carry, unroll=None):
    return lax.fori_loop(0, count, body, carry, unroll=count if unroll is None else unroll)


def kernel(
    nx, ny, load, material, table, out_x, out_r,
    v, vl, stress, moduli, compact, row_halo, col_send, col_halo, corner, mat_halo, slots_x, slots_y, own_sum,
    moments, send_sem, recv_sem, sum_send, sum_recv_x, sum_recv_y,
):
    rows, cols = load.shape[2], load.shape[3]
    tiles, planes = rows // 8, cols // 128
    mat_rows, mat_cols = material.shape[1], material.shape[2]
    extra = planes
    gx, gy = lax.axis_index("gx"), lax.axis_index("gy")
    has = {
        (-1, 0): gx > 0, (1, 0): gx < nx - 1, (0, -1): gy > 0, (0, 1): gy < ny - 1,
    }
    for dx, dy in DIAGONAL:
        has[dx, dy] = jnp.logical_and(has[dx, 0], has[0, dy])

    def at(dx, dy):
        return {"gx": lax.rem(gx + dx + nx, nx), "gy": lax.rem(gy + dy + ny, ny)}

    barrier = pltpu.get_barrier_semaphore()
    greeted = [(d, 0) for d in range(1, nx)] + [(0, d) for d in range(1, ny)] + DIAGONAL
    for way in greeted:
        pl.semaphore_signal(barrier, inc=1, device_id=at(*way), device_id_type=MESH)

    sub = lax.broadcasted_iota(jnp.int32, (8, 128), 0)
    lane = lax.broadcasted_iota(jnp.int32, (8, 128), 1)

    for c in range(2):
        col_send[0, c] = load[0, c, :, 0:128].T[0:8]
        col_send[1, c] = load[0, c, :, cols - 128 : cols].T[120:128]

    pl.semaphore_wait(barrier, len(greeted))

    def copies(index):
        dx, dy = WAYS[index]
        width = slice(0, cols) if dy == 0 else (slice(0, 128) if dy < 0 else slice(cols - 128, cols))
        strip = slice(0, 8) if dx < 0 else slice(rows - 8, rows)
        third = 1 - dy
        if dx == 0:
            mat_src, mat_rows_at = slice(0, mat_rows), slice(0, mat_rows)
            src = col_send.at[0 if dy < 0 else 1]
            dst = col_halo.at[:, slice(0, 8) if dy < 0 else slice(120, 128), :]
        else:
            mat_src = slice(0, 8) if dx < 0 else slice(mat_rows - 8, mat_rows)
            mat_rows_at = slice(mat_rows, mat_rows + 8) if dx < 0 else slice(mat_rows + 8, mat_rows + 16)
            src = load.at[0, :, strip, width]
            if dy == 0:
                dst = row_halo.at[0 if dx < 0 else 1]
            else:
                dst = corner.at[0 if dx < 0 else 1, 0 if dy > 0 else 1]
        field = pltpu.make_async_remote_copy(
            src_ref=src, dst_ref=dst, send_sem=send_sem.at[2 * index], recv_sem=recv_sem.at[2 * index],
            device_id=at(dx, dy), device_id_type=MESH,
        )
        classes = pltpu.make_async_remote_copy(
            src_ref=material.at[0, mat_src, :], dst_ref=mat_halo.at[third, mat_rows_at, :],
            send_sem=send_sem.at[2 * index + 1], recv_sem=recv_sem.at[2 * index + 1],
            device_id=at(dx, dy), device_id_type=MESH,
        )
        return field, classes

    order = sorted(range(len(WAYS)), key=lambda i: -abs(WAYS[i][0]) - abs(WAYS[i][1]) - abs(WAYS[i][1]))
    for index in order:
        @pl.when(has[WAYS[index]])
        def _(index=index):
            for copy in copies(index):
                copy.start()

    mean = 0.0
    for k in range(CLASSES):
        mean = mean + (table[0, k] + 3.0 * table[1, k])
    inv_s = jnp.full((8, 128), (SPREAD / CLASSES) * mean, jnp.float32)
    quarter = 0.25 / inv_s

    def looked_up(classes):
        lam = jnp.zeros(classes.shape, jnp.float32)
        mu = jnp.zeros(classes.shape, jnp.float32)
        for k in range(CLASSES):
            hit = classes == k
            lam = jnp.where(hit, table[0, k], lam)
            mu = jnp.where(hit, table[1, k], mu)
        return lam, mu

    spread_row = lax.broadcasted_iota(jnp.int32, (mat_cols, cols), 0)
    spread_col = lax.broadcasted_iota(jnp.int32, (mat_cols, cols), 1)
    spread = (spread_row == spread_col // TILE).astype(jnp.float32)

    def widened(classes):
        lam, mu = looked_up(classes)
        both = jnp.concatenate([lam, mu], axis=0)
        wide = jnp.dot(both, spread, precision=lax.Precision.HIGHEST, preferred_element_type=jnp.float32)
        return wide[: classes.shape[0]], wide[classes.shape[0] :]

    def put_moduli(place, lam, mu):
        k, r = place
        small = quarter * mu
        moduli[0, k, r, :] = quarter * lam
        moduli[1, k, r, :] = small + small
        moduli[2, k, r, :] = small

    lam, mu = widened(material[0])
    for t in range(tiles):
        for k in range(planes):
            part = slice(128 * k, 128 * (k + 1))
            put_moduli(
                (k, slice(8 * t, 8 * t + 8)),
                jnp.broadcast_to(lam[t : t + 1, part], (8, 128)),
                jnp.broadcast_to(mu[t : t + 1, part], (8, 128)),
            )

    def own(t, acc):
        r = pl.ds(pl.multiple_of(8 * t, 8), 8)
        for c in range(2):
            for k in range(planes):
                value = load[0, c, r, 128 * k : 128 * (k + 1)]
                v[0, c, k, r, :] = value
                acc = acc + value * value
        return acc

    moments[0] = loop(tiles, own, jnp.zeros((8, 128), jnp.float32))

    for index in range(len(WAYS)):
        dx, dy = WAYS[index]
        @pl.when(has[-dx, -dy])
        def _(index=index):
            for copy in copies(index):
                copy.wait_recv()

    low = sub < 4
    left_lanes = lane < 64
    inner_right = jnp.logical_and(lane < 4, has[0, 1])
    inner_left = jnp.logical_and(lane >= 124, has[0, -1])
    inner_lanes = jnp.logical_or(inner_right, inner_left)
    inner_below = jnp.logical_and(low, has[1, 0])
    inner_above = jnp.logical_and(sub >= 4, has[-1, 0])
    inner_subs = jnp.logical_or(inner_below, inner_above)
    inner_both = jnp.logical_and(inner_subs, inner_lanes)
    sub_mask = inner_subs.astype(jnp.float32)
    lane_mask = inner_lanes.astype(jnp.float32)
    both_mask = inner_both.astype(jnp.float32)
    halo = slice(rows, rows + 8)
    again = slice(rows + 8, rows + 16)
    for c in range(2):
        for k in range(planes):
            part = slice(128 * k, 128 * (k + 1))
            ring = jnp.where(low, row_halo[0, c, :, part], row_halo[1, c, :, part])
            v[0, c, k, halo, :] = jnp.where(inner_subs, ring, 0.0)
            v[0, c, k, again, :] = load[0, c, 0:8, part]
        beside = col_halo[c].T
        for t in range(tiles):
            value = jnp.where(inner_lanes, beside[8 * t : 8 * t + 8], 0.0)
            v[0, c, extra, 8 * t : 8 * t + 8, :] = value
            if t == 0:
                v[0, c, extra, again, :] = value
        below = jnp.where(left_lanes, corner[0, 1, c], corner[0, 0, c])
        above = jnp.where(left_lanes, corner[1, 1, c], corner[1, 0, c])
        v[0, c, extra, halo, :] = jnp.where(inner_both, jnp.where(low, below, above), 0.0)

    beyond = widened(mat_halo[1, mat_rows : mat_rows + 16, :])
    for k in range(planes):
        part = slice(128 * k, 128 * (k + 1))
        lam, mu = (
            jnp.where(
                inner_subs,
                jnp.where(low, jnp.broadcast_to(m[0:1, part], (8, 128)), jnp.broadcast_to(m[15:16, part], (8, 128))),
                0.0,
            )
            for m in beyond
        )
        put_moduli((k, halo), lam, mu)
    left, right = looked_up(mat_halo[0]), looked_up(mat_halo[2])
    for q in range(2):
        near = jnp.broadcast_to(right[q][:, 0:1], (mat_rows + 16, 128))
        far = jnp.broadcast_to(left[q][:, mat_cols - 1 : mat_cols], (mat_rows + 16, 128))
        wide_lane = lax.broadcasted_iota(jnp.int32, (mat_rows + 16, 128), 1)
        compact[q] = jnp.where(wide_lane < 64, near, far)
    for t in range(tiles):
        lam, mu = (
            jnp.where(inner_lanes, jnp.broadcast_to(compact[q, t : t + 1, :], (8, 128)), 0.0) for q in range(2)
        )
        put_moduli((extra, slice(8 * t, 8 * t + 8)), lam, mu)
    lam, mu = (
        jnp.where(
            inner_both,
            jnp.where(
                low,
                jnp.broadcast_to(compact[q, mat_rows : mat_rows + 1, :], (8, 128)),
                jnp.broadcast_to(compact[q, mat_rows + 15 : mat_rows + 16, :], (8, 128)),
            ),
            0.0,
        )
        for q in range(2)
    )
    put_moduli((extra, halo), lam, mu)

    last_lane, first_lane = lane == 127, lane == 0

    def shifted_left(parts):
        turned = [pltpu.roll(x, 127, 1) for x in parts]
        return [jnp.where(last_lane, turned[(k + 1) % SIDE], turned[k]) for k in range(SIDE)]

    def shifted_right(parts):
        turned = [pltpu.roll(x, 1, 1) for x in parts]
        return [jnp.where(first_lane, turned[k - 1], turned[k]) for k in range(SIDE)]

    def first_shift(t, carry):
        r = pl.ds(pl.multiple_of(8 * t, 8), 8)
        for c in range(2):
            for k, value in enumerate(shifted_left([v[0, c, k, r, :] for k in range(SIDE)])):
                vl[c, k, r, :] = value
        return carry

    loop(tiles + 2, first_shift, 0)

    def level_step(level, carry):
        diag = jnp.where(level == 0, 0.0, DIAG)

        def stresses(t, carry):
            base = pl.multiple_of(8 * t, 8)
            r, rr = pl.ds(base, 8), pl.ds(base + 1, 8)
            for k in range(SIDE):
                d = []
                for c in range(2):
                    u = vl[c, k, rr, :] - v[level, c, k, r, :]
                    w = v[level, c, k, rr, :] - vl[c, k, r, :]
                    d.append((u + w, u - w))
                (dx0, dy0), (dx1, dy1) = d
                common = moduli[0, k, r, :] * (dx0 + dy1)
                twice = moduli[1, k, r, :]
                s = pl.ds(base + 8, 8)
                stress[0, k, s, :] = common + twice * dx0
                stress[1, k, s, :] = moduli[2, k, r, :] * (dy0 + dx1)
                stress[2, k, s, :] = common + twice * dy1
            return carry

        loop(tiles + 1, stresses, 0)
        for q in range(3):
            for k in range(SIDE):
                stress[q, k, 0:8, :] = stress[q, k, rows + 8 : rows + 16, :]

        def forces(base, acc, border):
            r, s, b = pl.ds(base, 8), pl.ds(base + 8, 8), pl.ds(base + 7, 8)
            plain, moved = ([], []), ([], [])
            for k in range(SIDE):
                xx, xy, yy = stress[0, k, s, :], stress[1, k, s, :], stress[2, k, s, :]
                xx_b, xy_b, yy_b = stress[0, k, b, :], stress[1, k, b, :], stress[2, k, b, :]
                dxx, sxy, dxy, syy = xx_b - xx, xy_b + xy, xy_b - xy, yy_b + yy
                plain[0].append(dxx - sxy)
                moved[0].append(dxx + sxy)
                plain[1].append(dxy - syy)
                moved[1].append(dxy + syy)
            for c in range(2):
                new = []
                for k, value in enumerate(shifted_right(moved[c])):
                    old = v[level, c, k, r, :]
                    value = plain[c][k] + value + diag * old
                    if border:
                        value = value * (both_mask if k == extra else sub_mask)
                    elif k == extra:
                        value = value * lane_mask
                    else:
                        acc = (acc[0] + old * value, acc[1] + value * value)
                    v[level + 1, c, k, r, :] = value
                    new.append(value)
                for k, value in enumerate(shifted_left(new)):
                    vl[c, k, r, :] = value
            return acc

        zero = jnp.zeros((8, 128), jnp.float32)
        acc = loop(tiles, lambda t, acc: forces(pl.multiple_of(8 * t, 8), acc, False), (zero, zero))
        forces(rows, None, True)
        for c in range(2):
            for k in range(SIDE):
                v[level + 1, c, k, again, :] = v[level + 1, c, k, 0:8, :]
                vl[c, k, again, :] = vl[c, k, 0:8, :]
        moments[2 * level + 1] = acc[0]
        moments[2 * level + 2] = acc[1]
        return carry

    lax.fori_loop(0, LEVELS, level_step, 0)

    partial = jnp.sum(moments[0 : 2 * LEVELS], axis=1)
    partial = jnp.sum(partial, axis=1, keepdims=True)
    mine = jnp.sum(jnp.where(lane == sub, jnp.broadcast_to(partial, (8, 128)), 0.0), axis=0, keepdims=True)

    def summed(value, slots, here, size, way, first_sem, recv):
        slots[here] = value
        own_sum[first_sem] = value

        def copy(d):
            return pltpu.make_async_remote_copy(
                src_ref=own_sum.at[first_sem], dst_ref=slots.at[here],
                send_sem=sum_send.at[first_sem, d - 1], recv_sem=recv.at[d - 1],
                device_id=at(*way(d)), device_id_type=MESH,
            )

        for d in range(1, size):
            copy(d).start()
        for d in range(1, size):
            copy(d).wait_recv()
        total = slots[0]
        for d in range(1, size):
            total = total + slots[d]
        return total, copy

    mine, copy_x = summed(mine, slots_x, gx, nx, lambda d: (d, 0), 0, sum_recv_x)
    mine, copy_y = summed(mine, slots_y, gy, ny, lambda d: (0, d), 1, sum_recv_y)

    g = [jnp.broadcast_to(mine[:, k : k + 1], (8, 128)) for k in range(2 * LEVELS)]
    m = [g[0], g[1]]
    for k in range(2, 2 * LEVELS):
        m.append(g[k] + DIAG * m[k - 1])
    sigma0 = jnp.full((8, 128), MASS, jnp.float32)
    sigma = sigma0 + (CENTRE / SPREAD) * inv_s
    shift = [sigma0] + [sigma] * (2 * LEVELS - 2)
    rho, phi = dict(enumerate(m)), dict(enumerate(m))
    one, nil = jnp.ones((8, 128), jnp.float32), jnp.zeros((8, 128), jnp.float32)
    r_of, p_of, x_of = [one] + [nil] * LEVELS, [one] + [nil] * LEVELS, [nil] * LEVELS
    for t in range(ITERS):
        psi = {l: phi[l + 1] * inv_s + shift[l] * phi[l] for l in range(t, 2 * LEVELS - 1 - t)}
        alpha = rho[t] / psi[t]
        for k in range(t + 1):
            x_of[k] = x_of[k] + alpha * p_of[k]
        ap = [
            (p_of[k - 1] * inv_s if k else nil) + (shift[k] * p_of[k] if k <= t else nil) for k in range(t + 2)
        ]
        for k in range(t + 2):
            r_of[k] = r_of[k] - alpha * ap[k]
        if t + 1 < ITERS:
            new = {l: rho[l] - alpha * psi[l] for l in range(t + 1, 2 * LEVELS - 1 - t)}
            beta = -(alpha * inv_s) * new[t + 1] / rho[t]
            phi = {l: new[l] + beta * phi[l] for l in new}
            rho = new
            for k in range(t + 2):
                p_of[k] = r_of[k] + beta * p_of[k]

    def combine(t, carry):
        r = pl.ds(pl.multiple_of(8 * t, 8), 8)
        for c in range(2):
            for k in range(planes):
                basis = [v[l, c, k, r, :] for l in range(LEVELS + 1)]
                part = slice(128 * k, 128 * (k + 1))
                x = x_of[0] * basis[0]
                for l in range(1, LEVELS):
                    x = x + x_of[l] * basis[l]
                res = r_of[0] * basis[0]
                for l in range(1, LEVELS + 1):
                    res = res + r_of[l] * basis[l]
                out_x[0, c, r, part] = x
                out_r[0, c, r, part] = res
        return carry

    loop(tiles, combine, 0)

    for index in range(len(WAYS)):
        @pl.when(has[WAYS[index]])
        def _(index=index):
            for copy in copies(index):
                copy.wait_send()
    for d in range(1, nx):
        copy_x(d).wait_send()
    for d in range(1, ny):
        copy_y(d).wait_send()


def on_device(nx, ny, load, material, lame_table):
    rows, cols = load.shape[2], load.shape[3]
    mat_rows, mat_cols = material.shape[1], material.shape[2]
    planes = cols // 128
    vmem = pl.BlockSpec(memory_space=pltpu.VMEM)
    f32 = jnp.float32
    return pl.pallas_call(
        functools.partial(kernel, nx, ny),
        out_shape=[jax.ShapeDtypeStruct(load.shape, f32)] * 2,
        in_specs=[vmem, vmem, pl.BlockSpec(memory_space=pltpu.SMEM)],
        out_specs=[vmem, vmem],
        scratch_shapes=[
            pltpu.VMEM((LEVELS + 1, 2, planes + 1, rows + 16, 128), f32),
            pltpu.VMEM((2, planes + 1, rows + 16, 128), f32),
            pltpu.VMEM((3, planes + 1, rows + 16, 128), f32),
            pltpu.VMEM((3, planes + 1, rows + 8, 128), f32),
            pltpu.VMEM((2, mat_rows + 16, 128), f32),
            pltpu.VMEM((2, 2, 8, cols), f32),
            pltpu.VMEM((2, 2, 8, 128), f32),
            pltpu.VMEM((2, 128, rows), f32),
            pltpu.VMEM((2, 2, 2, 8, 128), f32),
            pltpu.VMEM((3, mat_rows + 16, mat_cols), jnp.int32),
            pltpu.VMEM((nx, 1, 128), f32),
            pltpu.VMEM((ny, 1, 128), f32),
            pltpu.VMEM((2, 1, 128), f32),
            pltpu.VMEM((2 * LEVELS + 1, 8, 128), f32),
            pltpu.SemaphoreType.DMA((2 * len(WAYS),)),
            pltpu.SemaphoreType.DMA((2 * len(WAYS),)),
            pltpu.SemaphoreType.DMA((2, max(nx, ny) - 1)),
            pltpu.SemaphoreType.DMA((nx - 1,)),
            pltpu.SemaphoreType.DMA((ny - 1,)),
        ],
        compiler_params=pltpu.CompilerParams(collective_id=0, has_side_effects=True),
    )(load, material, lame_table)


def solution(mesh):
    return jax.shard_map(
        functools.partial(on_device, mesh.shape["gx"], mesh.shape["gy"]),
        mesh=mesh,
        in_specs=(P("samp", None, "gx", "gy"), P("samp", "gx", "gy"), P()),
        out_specs=(P("samp", None, "gx", "gy"), P("samp", None, "gx", "gy")),
        check_vma=False,
    )
```

time: 177 us -> 34.6 us (0.20)
  blocking collectives: 67.4 us -> 0 us
  starting transfers between devices: 45.8 us -> 0 us
  Pallas kernels: 0 us -> 31.1 us
  other arithmetic: 21.8 us -> 0 us
  local copies, waits for them, and re-layouts: 18.1 us -> 2.72 us
  between operations: 14.6 us -> 0.65 us
  waiting for transfers between devices: 8.58 us -> 0 us
    all_to_all x4 -> x0, blocking collectives: 67.4 us -> none  [from_everyone(): lax.all_to_all(jnp.broadcast_to(array[None], (devices, *array.shape)), ax...]
    ppermute x18 -> x0, starting transfers between devices: 45.8 us -> none  [the longest x8 24.3 us: padded_2(): before = lax.ppermute(last, axis, up)]
    pallas_call x0 -> x1, Pallas kernels: none -> 31.1 us  [on_device(): pl.pallas_call(functools.partial(kernel, nx, ny), out_shape=[jax.ShapeDty...]
    broadcast_in_dim x8 -> x0, local copies, waits for them, and re-layouts: 13.1 us -> none  [the longest x4 13 us: expand(): jnp.broadcast_to(tiles[:, :, None, :, None], (count, rows, TILE, cols, TI...]
    reduce_sum x9 -> x0, other arithmetic: 8.7 us -> none  [the longest x4 7.56 us: on_device(): local_gamma = jnp.sum(residual * residual, axis=(1, 2, 3))]
    ppermute x18 -> x0, waiting for transfers between devices: 8.58 us -> none  [the longest x8 6.8 us: padded_2(): after = lax.ppermute(leading, axis, down)]
    concatenate x10 -> x0, other arithmetic: 6.87 us -> none  [the longest x4 5.32 us: in_one(): jnp.concatenate([a.reshape(-1) for a in arrays])]
    sub x5 -> x0, other arithmetic: 2.82 us -> none  [the longest x1 2.65 us: on_device(): residual = residual - alpha_b * q_vec]
  transfers between devices with their start and end apart: 18 -> 0, of which waited for: 3 -> 0; matrix products, arithmetic and copies ran while one was open for 4% -> 0% of each run, Pallas kernels for 0% -> 0%
where the time goes in v1:
time: 34.6 us; the launch traced here: 34.5 us
  Pallas kernels  31.1 us (90%)
  local copies, waits for them, and re-layouts  2.72 us (8%)
  between operations  0.65 us (2%)
    pallas_call x1, Pallas kernels, on_device(): pl.pallas_call(functools.partial(kernel, nx, ny), out_shape=[jax.ShapeDty...  31.1 us
    unnamed x4, local copies, waits for them, and re-layouts  2.72 us

profile of v1, /device:TPU:1, one launch (start us, length us, event | category | flops | bytes accessed | tf_op | source)
XLA Modules:
  0.0 34.5 jit_solution(15229975501337427161)
XLA Ops:
  0.6 31.1 %shard_map.50 = (f32[1,2,128,512]{3,2,1,0:T(8,128)}, f32[1,2,128,512]{3,2,1,0:T(8,128)}) custom-call(f32[1,2,128,512]{3,2,1,0:T(8,128)} %load.1, s32[1,16,64]{2,1,0:T(8,128)} %material.1, f32[2,8]{1,0:T(2,128)} %table.1), custom_call_target="tpu_custom_call" | custom-call | tf_op jit(solution)/shard_map/pallas_call | solution.py:399
  31.7 0.0 copy-start
  31.7 1.9 %copy.7 = f32[1,2,128,512]{3,2,1,0:T(8,128)} copy(f32[1,2,128,512]{3,2,1,0:T(8,128)} %get-tuple-element.4) | data formatting | bytes 1048576
  33.7 0.0 copy-done
  33.7 0.8 %copy.8 = f32[1,2,128,512]{3,2,1,0:T(8,128)} copy(f32[1,2,128,512]{3,2,1,0:T(8,128)S(1)} %copy-done) | data formatting | bytes 1048576
Async XLA Ops:
  31.7 1.9 %copy-start = (f32[1,2,128,512]{3,2,1,0:T(8,128)S(1)}, f32[1,2,128,512]{3,2,1,0:T(8,128)}, u32[]{:S(2)}) copy-start(f32[1,2,128,512]{3,2,1,0:T(8,128)} %get-tuple-element.5) | copy-start | bytes 1572868

commit v2 on v1

--- a/solution.py
+++ b/solution.py
@@ -26,9 +26,9 @@
 
 
 def kernel(
-    nx, ny, load, material, table, out_x, out_r,
-    v, vl, stress, moduli, compact, row_halo, col_send, col_halo, corner, mat_halo, slots_x, slots_y, own_sum,
-    moments, send_sem, recv_sem, sum_send, sum_recv_x, sum_recv_y,
+    nx, ny, load_in, material_in, table_in, out_x, out_r,
+    load, material, table, v, vl, stress, moduli, compact, row_halo, col_send, col_halo, corner, mat_halo, slots,
+    own_sum, moments, load_sem, send_sem, recv_sem, sum_send, sum_recv, met,
 ):
     rows, cols = load.shape[2], load.shape[3]
     tiles, planes = rows // 8, cols // 128
@@ -45,9 +45,16 @@
         return {"gx": lax.rem(gx + dx + nx, nx), "gy": lax.rem(gy + dy + ny, ny)}
 
     barrier = pltpu.get_barrier_semaphore()
-    greeted = [(d, 0) for d in range(1, nx)] + [(0, d) for d in range(1, ny)] + DIAGONAL
-    for way in greeted:
+    for way in WAYS:
         pl.semaphore_signal(barrier, inc=1, device_id=at(*way), device_id_type=MESH)
+    fetches = [
+        pltpu.make_async_copy(load_in, load, load_sem.at[0]),
+        pltpu.make_async_copy(material_in, material, load_sem.at[1]),
+        pltpu.make_async_copy(table_in, table, load_sem.at[2]),
+    ]
+    for fetch in fetches:
+        fetch.start()
+    fetches[0].wait()
 
     sub = lax.broadcasted_iota(jnp.int32, (8, 128), 0)
     lane = lax.broadcasted_iota(jnp.int32, (8, 128), 1)
@@ -56,7 +63,8 @@
         col_send[0, c] = load[0, c, :, 0:128].T[0:8]
         col_send[1, c] = load[0, c, :, cols - 128 : cols].T[120:128]
 
-    pl.semaphore_wait(barrier, len(greeted))
+    fetches[1].wait()
+    pl.semaphore_wait(barrier, len(WAYS))
 
     def copies(index):
         dx, dy = WAYS[index]
@@ -93,6 +101,10 @@
             for copy in copies(index):
                 copy.start()
 
+    for way in WAYS:
+        pl.semaphore_signal(met.at[0], inc=1, device_id=at(*way), device_id_type=MESH)
+
+    fetches[2].wait()
     mean = 0.0
     for k in range(CLASSES):
         mean = mean + (table[0, k] + 3.0 * table[1, k])
@@ -145,6 +157,25 @@
         return acc
 
     moments[0] = loop(tiles, own, jnp.zeros((8, 128), jnp.float32))
+
+    last_lane, first_lane = lane == 127, lane == 0
+
+    def shifted_left(parts):
+        turned = [pltpu.roll(x, 127, 1) for x in parts]
+        return [jnp.where(last_lane, turned[(k + 1) % len(parts)], turned[k]) for k in range(len(parts))]
+
+    def shifted_right(parts):
+        turned = [pltpu.roll(x, 1, 1) for x in parts]
+        return [jnp.where(first_lane, turned[k - 1], turned[k]) for k in range(len(parts))]
+
+    def first_shift(t, carry):
+        r = pl.ds(pl.multiple_of(8 * t, 8), 8)
+        for c in range(2):
+            for k, value in enumerate(shifted_left([v[0, c, k, r, :] for k in range(planes)])[:-1]):
+                vl[c, k, r, :] = value
+        return carry
+
+    loop(tiles, first_shift, 0)
 
     for index in range(len(WAYS)):
         dx, dy = WAYS[index]
@@ -164,7 +195,6 @@
     inner_both = jnp.logical_and(inner_subs, inner_lanes)
     sub_mask = inner_subs.astype(jnp.float32)
     lane_mask = inner_lanes.astype(jnp.float32)
-    both_mask = inner_both.astype(jnp.float32)
     halo = slice(rows, rows + 8)
     again = slice(rows + 8, rows + 16)
     for c in range(2):
@@ -220,24 +250,32 @@
     )
     put_moduli((extra, halo), lam, mu)
 
-    last_lane, first_lane = lane == 127, lane == 0
-
-    def shifted_left(parts):
-        turned = [pltpu.roll(x, 127, 1) for x in parts]
-        return [jnp.where(last_lane, turned[(k + 1) % SIDE], turned[k]) for k in range(SIDE)]
-
-    def shifted_right(parts):
-        turned = [pltpu.roll(x, 1, 1) for x in parts]
-        return [jnp.where(first_lane, turned[k - 1], turned[k]) for k in range(SIDE)]
-
-    def first_shift(t, carry):
+    def rest_shift(t, carry):
         r = pl.ds(pl.multiple_of(8 * t, 8), 8)
         for c in range(2):
-            for k, value in enumerate(shifted_left([v[0, c, k, r, :] for k in range(SIDE)])):
-                vl[c, k, r, :] = value
+            near, far, start = (v[0, c, k, r, :] for k in (planes - 1, extra, 0))
+            for k, value in enumerate(shifted_left([near, far, start])[:-1]):
+                vl[c, planes - 1 + k, r, :] = value
         return carry
 
-    loop(tiles + 2, first_shift, 0)
+    loop(tiles, rest_shift, 0)
+    for c in range(2):
+        for k, value in enumerate(shifted_left([v[0, c, k, halo, :] for k in range(SIDE)])):
+            vl[c, k, halo, :] = value
+        for k in range(SIDE):
+            vl[c, k, again, :] = vl[c, k, 0:8, :]
+
+    beyond_edge = jnp.logical_and(last_lane, jnp.logical_not(has[0, 1]))
+    edge_mask = jnp.where(beyond_edge, 0.0, 1.0)
+    moved_lanes = jnp.logical_or(
+        jnp.logical_or(jnp.logical_and(lane < 3, has[0, 1]), last_lane),
+        jnp.logical_and(jnp.logical_and(lane >= 123, lane < 127), has[0, -1]),
+    )
+    moved_mask = moved_lanes.astype(jnp.float32)
+
+    pl.semaphore_wait(met.at[0], len(WAYS))
+    for dx, dy in WAYS:
+        pl.semaphore_signal(met.at[1], inc=1, device_id=at(2 * dx, 2 * dy), device_id_type=MESH)
 
     def level_step(level, carry):
         diag = jnp.where(level == 0, 0.0, DIAG)
@@ -277,20 +315,22 @@
                 plain[1].append(dxy - syy)
                 moved[1].append(dxy + syy)
             for c in range(2):
-                new = []
-                for k, value in enumerate(shifted_right(moved[c])):
+                here = shifted_right(moved[c])
+                there = shifted_left(plain[c])
+                for k in range(SIDE):
                     old = v[level, c, k, r, :]
-                    value = plain[c][k] + value + diag * old
+                    value = plain[c][k] + here[k] + diag * old
+                    after = there[k] + moved[c][k] + diag * vl[c, k, r, :]
                     if border:
-                        value = value * (both_mask if k == extra else sub_mask)
-                    elif k == extra:
-                        value = value * lane_mask
-                    else:
+                        value, after = value * sub_mask, after * sub_mask
+                    if k == extra:
+                        value, after = value * lane_mask, after * moved_mask
+                    elif k == extra - 1:
+                        after = after * edge_mask
+                    if k < extra and not border:
                         acc = (acc[0] + old * value, acc[1] + value * value)
                     v[level + 1, c, k, r, :] = value
-                    new.append(value)
-                for k, value in enumerate(shifted_left(new)):
-                    vl[c, k, r, :] = value
+                    vl[c, k, r, :] = after
             return acc
 
         zero = jnp.zeros((8, 128), jnp.float32)
@@ -309,29 +349,23 @@
     partial = jnp.sum(moments[0 : 2 * LEVELS], axis=1)
     partial = jnp.sum(partial, axis=1, keepdims=True)
     mine = jnp.sum(jnp.where(lane == sub, jnp.broadcast_to(partial, (8, 128)), 0.0), axis=0, keepdims=True)
-
-    def summed(value, slots, here, size, way, first_sem, recv):
-        slots[here] = value
-        own_sum[first_sem] = value
-
-        def copy(d):
-            return pltpu.make_async_remote_copy(
-                src_ref=own_sum.at[first_sem], dst_ref=slots.at[here],
-                send_sem=sum_send.at[first_sem, d - 1], recv_sem=recv.at[d - 1],
-                device_id=at(*way(d)), device_id_type=MESH,
-            )
-
-        for d in range(1, size):
-            copy(d).start()
-        for d in range(1, size):
-            copy(d).wait_recv()
-        total = slots[0]
-        for d in range(1, size):
-            total = total + slots[d]
-        return total, copy
-
-    mine, copy_x = summed(mine, slots_x, gx, nx, lambda d: (d, 0), 0, sum_recv_x)
-    mine, copy_y = summed(mine, slots_y, gy, ny, lambda d: (0, d), 1, sum_recv_y)
+    me = gx * ny + gy
+    own_sum[0] = mine
+    slots[me] = mine
+    pl.semaphore_wait(met.at[1], len(WAYS))
+    peers = [(a, b) for a in range(nx) for b in range(ny) if a or b]
+    peers.sort(key=lambda w: -2 * min(w[1], ny - w[1]) - min(w[0], nx - w[0]))
+    for way in peers:
+        pltpu.make_async_remote_copy(
+            src_ref=own_sum.at[0], dst_ref=slots.at[me], send_sem=sum_send.at[0], recv_sem=sum_recv.at[0],
+            device_id=at(*way), device_id_type=MESH,
+        ).start()
+    everything = pltpu.make_async_remote_copy(
+        src_ref=slots.at[0 : nx * ny - 1], dst_ref=slots.at[0 : nx * ny - 1],
+        send_sem=sum_send.at[0], recv_sem=sum_recv.at[0], device_id=at(1, 0), device_id_type=MESH,
+    )
+    everything.wait_recv()
+    mine = jnp.sum(slots[...], axis=0)
 
     g = [jnp.broadcast_to(mine[:, k : k + 1], (8, 128)) for k in range(2 * LEVELS)]
     m = [g[0], g[1]]
@@ -384,10 +418,7 @@
         def _(index=index):
             for copy in copies(index):
                 copy.wait_send()
-    for d in range(1, nx):
-        copy_x(d).wait_send()
-    for d in range(1, ny):
-        copy_y(d).wait_send()
+    everything.wait_send()
 
 
 def on_device(nx, ny, load, material, lame_table):
@@ -399,9 +430,12 @@
     return pl.pallas_call(
         functools.partial(kernel, nx, ny),
         out_shape=[jax.ShapeDtypeStruct(load.shape, f32)] * 2,
-        in_specs=[vmem, vmem, pl.BlockSpec(memory_space=pltpu.SMEM)],
+        in_specs=[pl.BlockSpec(memory_space=pltpu.HBM)] * 3,
         out_specs=[vmem, vmem],
         scratch_shapes=[
+            pltpu.VMEM(load.shape, f32),
+            pltpu.VMEM(material.shape, jnp.int32),
+            pltpu.SMEM(lame_table.shape, f32),
             pltpu.VMEM((LEVELS + 1, 2, planes + 1, rows + 16, 128), f32),
             pltpu.VMEM((2, planes + 1, rows + 16, 128), f32),
             pltpu.VMEM((3, planes + 1, rows + 16, 128), f32),
@@ -412,18 +446,20 @@
             pltpu.VMEM((2, 128, rows), f32),
             pltpu.VMEM((2, 2, 2, 8, 128), f32),
             pltpu.VMEM((3, mat_rows + 16, mat_cols), jnp.int32),
-            pltpu.VMEM((nx, 1, 128), f32),
-            pltpu.VMEM((ny, 1, 128), f32),
-            pltpu.VMEM((2, 1, 128), f32),
+            pltpu.VMEM((nx * ny, 1, 128), f32),
+            pltpu.VMEM((1, 1, 128), f32),
             pltpu.VMEM((2 * LEVELS + 1, 8, 128), f32),
+            pltpu.SemaphoreType.DMA((3,)),
             pltpu.SemaphoreType.DMA((2 * len(WAYS),)),
             pltpu.SemaphoreType.DMA((2 * len(WAYS),)),
-            pltpu.SemaphoreType.DMA((2, max(nx, ny) - 1)),
-            pltpu.SemaphoreType.DMA((nx - 1,)),
-            pltpu.SemaphoreType.DMA((ny - 1,)),
+            pltpu.SemaphoreType.DMA((1,)),
+            pltpu.SemaphoreType.DMA((1,)),
+            pltpu.SemaphoreType.REGULAR((2,)),
         ],
-        compiler_params=pltpu.CompilerParams(collective_id=0, has_side_effects=True),
-    )(load, material, lame_table)
+        compiler_params=pltpu.CompilerParams(
+            collective_id=0, has_side_effects=True, vmem_limit_bytes=24 * 1024 * 1024
+        ),
+    )(*(pltpu.with_memory_space_constraint(a, pltpu.HBM) for a in (load, material, lame_table)))
 
 
 def solution(mesh):

time: 34.6 us -> 25.1 us (0.73)
  Pallas kernels: 31.1 us -> 22.8 us
  local copies, waits for them, and re-layouts: 2.72 us -> 1.59 us
    pallas_call x1, Pallas kernels: 31.1 us -> 22.8 us  [on_device(): pl.pallas_call(functools.partial(kernel, nx, ny), out_shape=[jax.ShapeDty...]
    unnamed x4 -> x2, local copies, waits for them, and re-layouts: 2.72 us -> 1.59 us
where the time goes in v2:
time: 25.1 us; the launch traced here: 25 us
  Pallas kernels  22.8 us (91%)
  local copies, waits for them, and re-layouts  1.59 us (6%)
  between operations  0.64 us (3%)
    pallas_call x1, Pallas kernels, on_device(): pl.pallas_call(functools.partial(kernel, nx, ny), out_shape=[jax.ShapeDty...  22.8 us
    unnamed x2, local copies, waits for them, and re-layouts  1.59 us

profile of v2, /device:TPU:1, one launch (start us, length us, event | category | flops | bytes accessed | tf_op | source)
XLA Modules:
  0.0 25.0 jit_solution(12697337135953962766)
XLA Ops:
  0.6 22.8 %shard_map.50 = (f32[1,2,128,512]{3,2,1,0:T(8,128)S(1)}, f32[1,2,128,512]{3,2,1,0:T(8,128)S(1)}) custom-call(f32[1,2,128,512]{3,2,1,0:T(8,128)} %load_in.1, s32[1,16,64]{2,1,0:T(8,128)} %material_in.1, f32[2,8]{1,0:T(2,128)} %table_in.1), custom_call_target="tpu_custom_call" | custom-call | tf_op jit(solution)/shard_map/pallas_call | solution.py:430
  23.4 0.8 %copy.7 = f32[1,2,128,512]{3,2,1,0:T(8,128)} copy(f32[1,2,128,512]{3,2,1,0:T(8,128)S(1)} %get-tuple-element.4) | data formatting | bytes 1048576
  24.2 0.8 %copy.8 = f32[1,2,128,512]{3,2,1,0:T(8,128)} copy(f32[1,2,128,512]{3,2,1,0:T(8,128)S(1)} %get-tuple-element.5) | data formatting | bytes 1048576

commit v3 on v2

--- a/solution.py
+++ b/solution.py
@@ -18,6 +18,7 @@
 MESH = pl.DeviceIdType.MESH
 WAYS = [(dx, dy) for dx in (-1, 0, 1) for dy in (-1, 0, 1) if (dx, dy) != (0, 0)]
 SIDE = 5
+PIECES = 4
 DIAGONAL = [w for w in WAYS if w[0] and w[1]]
 
 
@@ -26,8 +27,8 @@
 
 
 def kernel(
-    nx, ny, load_in, material_in, table_in, out_x, out_r,
-    load, material, table, v, vl, stress, moduli, compact, row_halo, col_send, col_halo, corner, mat_halo, slots,
+    nx, ny, load_in, material_in, table_in, v, factors,
+    load, material, table, vl, stress, moduli, compact, row_halo, col_send, col_halo, corner, mat_halo, slots,
     own_sum, moments, load_sem, send_sem, recv_sem, sum_send, sum_recv, met,
 ):
     rows, cols = load.shape[2], load.shape[3]
@@ -44,16 +45,17 @@
     def at(dx, dy):
         return {"gx": lax.rem(gx + dx + nx, nx), "gy": lax.rem(gy + dy + ny, ny)}
 
-    barrier = pltpu.get_barrier_semaphore()
-    for way in WAYS:
-        pl.semaphore_signal(barrier, inc=1, device_id=at(*way), device_id_type=MESH)
     fetches = [
         pltpu.make_async_copy(load_in, load, load_sem.at[0]),
         pltpu.make_async_copy(material_in, material, load_sem.at[1]),
         pltpu.make_async_copy(table_in, table, load_sem.at[2]),
     ]
-    for fetch in fetches:
-        fetch.start()
+    fetches[0].start()
+    barrier = pltpu.get_barrier_semaphore()
+    for way in WAYS:
+        pl.semaphore_signal(barrier, inc=1, device_id=at(*way), device_id_type=MESH)
+    fetches[1].start()
+    fetches[2].start()
     fetches[0].wait()
 
     sub = lax.broadcasted_iota(jnp.int32, (8, 128), 0)
@@ -277,10 +279,8 @@
     for dx, dy in WAYS:
         pl.semaphore_signal(met.at[1], inc=1, device_id=at(2 * dx, 2 * dy), device_id_type=MESH)
 
-    def level_step(level, carry):
-        diag = jnp.where(level == 0, 0.0, DIAG)
-
-        def stresses(t, carry):
+    def stresses(level, tally):
+        def body(t, energy):
             base = pl.multiple_of(8 * t, 8)
             r, rr = pl.ds(base, 8), pl.ds(base + 1, 8)
             for k in range(SIDE):
@@ -290,61 +290,79 @@
                     w = v[level, c, k, rr, :] - vl[c, k, r, :]
                     d.append((u + w, u - w))
                 (dx0, dy0), (dx1, dy1) = d
-                common = moduli[0, k, r, :] * (dx0 + dy1)
+                volume, shear = dx0 + dy1, dy0 + dx1
+                common = moduli[0, k, r, :] * volume
                 twice = moduli[1, k, r, :]
+                xx, xy, yy = common + twice * dx0, moduli[2, k, r, :] * shear, common + twice * dy1
+                if tally and k < extra:
+                    energy = energy + (xx * dx0 + yy * dy1 + xy * shear)
                 s = pl.ds(base + 8, 8)
-                stress[0, k, s, :] = common + twice * dx0
-                stress[1, k, s, :] = moduli[2, k, r, :] * (dy0 + dx1)
-                stress[2, k, s, :] = common + twice * dy1
-            return carry
-
-        loop(tiles + 1, stresses, 0)
+                stress[0, k, s, :] = xx
+                stress[1, k, s, :] = xy
+                stress[2, k, s, :] = yy
+            return energy
+
+        energy = loop(tiles, body, jnp.zeros((8, 128), jnp.float32))
+        tally = False
+        body(tiles, energy)
         for q in range(3):
             for k in range(SIDE):
                 stress[q, k, 0:8, :] = stress[q, k, rows + 8 : rows + 16, :]
-
-        def forces(base, acc, border):
-            r, s, b = pl.ds(base, 8), pl.ds(base + 8, 8), pl.ds(base + 7, 8)
-            plain, moved = ([], []), ([], [])
-            for k in range(SIDE):
-                xx, xy, yy = stress[0, k, s, :], stress[1, k, s, :], stress[2, k, s, :]
-                xx_b, xy_b, yy_b = stress[0, k, b, :], stress[1, k, b, :], stress[2, k, b, :]
-                dxx, sxy, dxy, syy = xx_b - xx, xy_b + xy, xy_b - xy, yy_b + yy
-                plain[0].append(dxx - sxy)
-                moved[0].append(dxx + sxy)
-                plain[1].append(dxy - syy)
-                moved[1].append(dxy + syy)
-            for c in range(2):
-                here = shifted_right(moved[c])
-                there = shifted_left(plain[c])
-                for k in range(SIDE):
-                    old = v[level, c, k, r, :]
-                    value = plain[c][k] + here[k] + diag * old
-                    after = there[k] + moved[c][k] + diag * vl[c, k, r, :]
-                    if border:
-                        value, after = value * sub_mask, after * sub_mask
-                    if k == extra:
-                        value, after = value * lane_mask, after * moved_mask
-                    elif k == extra - 1:
-                        after = after * edge_mask
-                    if k < extra and not border:
-                        acc = (acc[0] + old * value, acc[1] + value * value)
+        return energy
+
+    def forces(level, base, acc, border, final):
+        r, s, b = pl.ds(base, 8), pl.ds(base + 8, 8), pl.ds(base + 7, 8)
+        plain, moved = ([], []), ([], [])
+        for k in range(SIDE):
+            xx, xy, yy = stress[0, k, s, :], stress[1, k, s, :], stress[2, k, s, :]
+            xx_b, xy_b, yy_b = stress[0, k, b, :], stress[1, k, b, :], stress[2, k, b, :]
+            dxx, sxy, dxy, syy = xx_b - xx, xy_b + xy, xy_b - xy, yy_b + yy
+            plain[0].append(dxx - sxy)
+            moved[0].append(dxx + sxy)
+            plain[1].append(dxy - syy)
+            moved[1].append(dxy + syy)
+        for c in range(2):
+            here = shifted_right(moved[c])
+            there = None if final else shifted_left(plain[c])
+            for k in range(planes if final else SIDE):
+                old = v[level, c, k, r, :]
+                value = plain[c][k] + here[k]
+                if level:
+                    value = value - old
+                if final:
                     v[level + 1, c, k, r, :] = value
-                    vl[c, k, r, :] = after
-            return acc
-
-        zero = jnp.zeros((8, 128), jnp.float32)
-        acc = loop(tiles, lambda t, acc: forces(pl.multiple_of(8 * t, 8), acc, False), (zero, zero))
-        forces(rows, None, True)
+                    continue
+                after = there[k] + moved[c][k]
+                if level:
+                    after = after - vl[c, k, r, :]
+                if border:
+                    value, after = value * sub_mask, after * sub_mask
+                if k == extra:
+                    value, after = value * lane_mask, after * moved_mask
+                elif k == extra - 1:
+                    after = after * edge_mask
+                if k < extra and not border:
+                    acc = (acc[0] + old * value, acc[1] + value * value)
+                v[level + 1, c, k, r, :] = value
+                vl[c, k, r, :] = after
+        return acc
+
+    zero = jnp.zeros((8, 128), jnp.float32)
+    for level in range(LEVELS - 1):
+        stresses(level, False)
+        acc = loop(
+            tiles,
+            lambda t, acc, level=level: forces(level, pl.multiple_of(8 * t, 8), acc, False, False),
+            (zero, zero),
+        )
+        forces(level, rows, None, True, False)
         for c in range(2):
             for k in range(SIDE):
                 v[level + 1, c, k, again, :] = v[level + 1, c, k, 0:8, :]
                 vl[c, k, again, :] = vl[c, k, 0:8, :]
         moments[2 * level + 1] = acc[0]
         moments[2 * level + 2] = acc[1]
-        return carry
-
-    lax.fori_loop(0, LEVELS, level_step, 0)
+    moments[2 * LEVELS - 1] = stresses(LEVELS - 1, True) + DIAG * moments[2 * LEVELS - 2]
 
     partial = jnp.sum(moments[0 : 2 * LEVELS], axis=1)
     partial = jnp.sum(partial, axis=1, keepdims=True)
@@ -364,6 +382,12 @@
         src_ref=slots.at[0 : nx * ny - 1], dst_ref=slots.at[0 : nx * ny - 1],
         send_sem=sum_send.at[0], recv_sem=sum_recv.at[0], device_id=at(1, 0), device_id_type=MESH,
     )
+
+    def final_forces(t, carry):
+        forces(LEVELS - 1, pl.multiple_of(8 * t, 8), None, False, True)
+        return carry
+
+    loop(tiles, final_forces, 0)
     everything.wait_recv()
     mine = jnp.sum(slots[...], axis=0)
 
@@ -395,23 +419,10 @@
             for k in range(t + 2):
                 p_of[k] = r_of[k] + beta * p_of[k]
 
-    def combine(t, carry):
-        r = pl.ds(pl.multiple_of(8 * t, 8), 8)
-        for c in range(2):
-            for k in range(planes):
-                basis = [v[l, c, k, r, :] for l in range(LEVELS + 1)]
-                part = slice(128 * k, 128 * (k + 1))
-                x = x_of[0] * basis[0]
-                for l in range(1, LEVELS):
-                    x = x + x_of[l] * basis[l]
-                res = r_of[0] * basis[0]
-                for l in range(1, LEVELS + 1):
-                    res = res + r_of[l] * basis[l]
-                out_x[0, c, r, part] = x
-                out_r[0, c, r, part] = res
-        return carry
-
-    loop(tiles, combine, 0)
+    for k in range(LEVELS):
+        factors[k] = x_of[k]
+    for k in range(LEVELS + 1):
+        factors[LEVELS + k] = r_of[k]
 
     for index in range(len(WAYS)):
         @pl.when(has[WAYS[index]])
@@ -421,22 +432,58 @@
     everything.wait_send()
 
 
+def combine(v, factors, out_x, out_r, x_part, r_part, sems):
+    rows, cols = out_x.shape[2], out_x.shape[3]
+    planes = cols // 128
+    x_of = [factors[k] for k in range(LEVELS)]
+    r_of = [factors[LEVELS + k] for k in range(LEVELS + 1)]
+    size = rows // PIECES
+    copies = []
+    for piece in range(PIECES):
+        def body(t, carry):
+            r = pl.ds(pl.multiple_of(piece * size + 8 * t, 8), 8)
+            for c in range(2):
+                for k in range(planes):
+                    basis = [v[l, c, k, r, :] for l in range(LEVELS + 1)]
+                    part = slice(128 * k, 128 * (k + 1))
+                    x = x_of[0] * basis[0]
+                    for l in range(1, LEVELS):
+                        x = x + x_of[l] * basis[l]
+                    res = r_of[0] * basis[0]
+                    for l in range(1, LEVELS + 1):
+                        res = res + r_of[l] * basis[l]
+                    x_part[0, c, r, part] = x
+                    r_part[0, c, r, part] = res
+            return carry
+
+        loop(size // 8, body, 0)
+        here = pl.ds(piece * size, size)
+        for i, (source, target) in enumerate(((x_part, out_x), (r_part, out_r))):
+            copy = pltpu.make_async_copy(source.at[0, :, here, :], target.at[0, :, here, :], sems.at[i, piece])
+            copy.start()
+            copies.append(copy)
+    for copy in copies:
+        copy.wait()
+
+
 def on_device(nx, ny, load, material, lame_table):
     rows, cols = load.shape[2], load.shape[3]
     mat_rows, mat_cols = material.shape[1], material.shape[2]
     planes = cols // 128
     vmem = pl.BlockSpec(memory_space=pltpu.VMEM)
     f32 = jnp.float32
-    return pl.pallas_call(
+    v, factors = pl.pallas_call(
         functools.partial(kernel, nx, ny),
-        out_shape=[jax.ShapeDtypeStruct(load.shape, f32)] * 2,
+        out_shape=[
+            jax.ShapeDtypeStruct((LEVELS + 1, 2, planes + 1, rows + 16, 128), f32),
+            jax.ShapeDtypeStruct((2 * LEVELS + 1, 8, 128), f32),
+        ],
         in_specs=[pl.BlockSpec(memory_space=pltpu.HBM)] * 3,
         out_specs=[vmem, vmem],
         scratch_shapes=[
             pltpu.VMEM(load.shape, f32),
             pltpu.VMEM(material.shape, jnp.int32),
             pltpu.SMEM(lame_table.shape, f32),
-            pltpu.VMEM((LEVELS + 1, 2, planes + 1, rows + 16, 128), f32),
             pltpu.VMEM((2, planes + 1, rows + 16, 128), f32),
             pltpu.VMEM((3, planes + 1, rows + 16, 128), f32),
             pltpu.VMEM((3, planes + 1, rows + 8, 128), f32),
@@ -448,7 +495,7 @@
             pltpu.VMEM((3, mat_rows + 16, mat_cols), jnp.int32),
             pltpu.VMEM((nx * ny, 1, 128), f32),
             pltpu.VMEM((1, 1, 128), f32),
-            pltpu.VMEM((2 * LEVELS + 1, 8, 128), f32),
+            pltpu.VMEM((2 * LEVELS, 8, 128), f32),
             pltpu.SemaphoreType.DMA((3,)),
             pltpu.SemaphoreType.DMA((2 * len(WAYS),)),
             pltpu.SemaphoreType.DMA((2 * len(WAYS),)),
@@ -460,6 +507,16 @@
             collective_id=0, has_side_effects=True, vmem_limit_bytes=24 * 1024 * 1024
         ),
     )(*(pltpu.with_memory_space_constraint(a, pltpu.HBM) for a in (load, material, lame_table)))
+    return pl.pallas_call(
+        combine,
+        out_shape=[jax.ShapeDtypeStruct(load.shape, f32)] * 2,
+        in_specs=[vmem, vmem],
+        out_specs=[pl.BlockSpec(memory_space=pltpu.HBM)] * 2,
+        scratch_shapes=[
+            pltpu.VMEM(load.shape, f32), pltpu.VMEM(load.shape, f32), pltpu.SemaphoreType.DMA((2, PIECES)),
+        ],
+        compiler_params=pltpu.CompilerParams(vmem_limit_bytes=24 * 1024 * 1024),
+    )(v, factors)
 
 
 def solution(mesh):

time: 25.1 us -> 23.4 us (0.932)
  local copies, waits for them, and re-layouts: 1.59 us -> 0 us
    unnamed x2 -> x0, local copies, waits for them, and re-layouts: 1.59 us -> none
    pallas_call x1, Pallas kernels: 22.8 us -> 21.6 us  [on_device(): pl.pallas_call(functools.partial(kernel, nx, ny), out_shape=[jax.ShapeDty...]
    pallas_call x0 -> x1, Pallas kernels: none -> 1.07 us  [on_device(): pl.pallas_call(combine, out_shape=[jax.ShapeDtypeStruct(load.shape, f32)]...]
where the time goes in v3:
time: 23.4 us; the launch traced here: 23.3 us
  Pallas kernels  22.6 us (97%)
  between operations  0.64 us (3%)
    pallas_call x1, Pallas kernels, on_device(): pl.pallas_call(functools.partial(kernel, nx, ny), out_shape=[jax.ShapeDty...  21.6 us
    pallas_call x1, Pallas kernels, on_device(): pl.pallas_call(combine, out_shape=[jax.ShapeDtypeStruct(load.shape, f32)]...  1.07 us

profile of v3, /device:TPU:1, one launch (start us, length us, event | category | flops | bytes accessed | tf_op | source)
XLA Modules:
  0.0 23.3 jit_solution(2574280575497631533)
XLA Ops:
  0.6 21.6 %shard_map.50 = (f32[5,2,5,144,128]{4,3,2,1,0:T(8,128)S(1)}, f32[9,8,128]{2,1,0:T(8,128)S(1)}) custom-call(f32[1,2,128,512]{3,2,1,0:T(8,128)} %load_in.1, s32[1,16,64]{2,1,0:T(8,128)} %material_in.1, f32[2,8]{1,0:T(2,128)} %table_in.1), custom_call_target="tpu_custom_call" | custom-call | tf_op jit(solution)/shard_map/pallas_call | solution.py:475
  22.2 1.1 %shard_map.51 = (f32[1,2,128,512]{3,2,1,0:T(8,128)}, f32[1,2,128,512]{3,2,1,0:T(8,128)}) custom-call(f32[5,2,5,144,128]{4,3,2,1,0:T(8,128)S(1)} %get-tuple-element.4.v, f32[9,8,128]{2,1,0:T(8,128)S(1)} %get-tuple-element.5.factors), custom_call_target="tpu_custom_call" | custom-call | tf_op jit(solution)/shard_map/pallas_call | solution.py:510

commit v4 on v3

--- a/solution.py
+++ b/solution.py
@@ -166,25 +166,14 @@
         turned = [pltpu.roll(x, 127, 1) for x in parts]
         return [jnp.where(last_lane, turned[(k + 1) % len(parts)], turned[k]) for k in range(len(parts))]
 
-    def shifted_right(parts):
-        turned = [pltpu.roll(x, 1, 1) for x in parts]
-        return [jnp.where(first_lane, turned[k - 1], turned[k]) for k in range(len(parts))]
-
     def first_shift(t, carry):
         r = pl.ds(pl.multiple_of(8 * t, 8), 8)
         for c in range(2):
-            for k, value in enumerate(shifted_left([v[0, c, k, r, :] for k in range(planes)])[:-1]):
+            for k, value in enumerate(shifted_left([v[0, c, k, r, :] for k in range(planes)])):
                 vl[c, k, r, :] = value
         return carry
 
     loop(tiles, first_shift, 0)
-
-    for index in range(len(WAYS)):
-        dx, dy = WAYS[index]
-        @pl.when(has[-dx, -dy])
-        def _(index=index):
-            for copy in copies(index):
-                copy.wait_recv()
 
     low = sub < 4
     left_lanes = lane < 64
@@ -197,24 +186,167 @@
     inner_both = jnp.logical_and(inner_subs, inner_lanes)
     sub_mask = inner_subs.astype(jnp.float32)
     lane_mask = inner_lanes.astype(jnp.float32)
+    beyond_edge = jnp.logical_and(last_lane, jnp.logical_not(has[0, 1]))
+    edge_mask = jnp.where(beyond_edge, 0.0, 1.0)
+    moved_lanes = jnp.logical_or(
+        jnp.logical_or(jnp.logical_and(lane < 3, has[0, 1]), last_lane),
+        jnp.logical_and(jnp.logical_and(lane >= 123, lane < 127), has[0, -1]),
+    )
+    moved_mask = moved_lanes.astype(jnp.float32)
     halo = slice(rows, rows + 8)
     again = slice(rows + 8, rows + 16)
+    zero = jnp.zeros((8, 128), jnp.float32)
+    everywhere = tuple(range(SIDE))
+
+    def stresses(level, base, where, energy=None):
+        r, rr, s = pl.ds(base, 8), pl.ds(base + 1, 8), pl.ds(base + 8, 8)
+        for k in where:
+            d = []
+            for c in range(2):
+                u = vl[c, k, rr, :] - v[level, c, k, r, :]
+                w = v[level, c, k, rr, :] - vl[c, k, r, :]
+                d.append((u + w, u - w))
+            (dx0, dy0), (dx1, dy1) = d
+            volume, shear = dx0 + dy1, dy0 + dx1
+            common = moduli[0, k, r, :] * volume
+            twice = moduli[1, k, r, :]
+            xx, xy, yy = common + twice * dx0, moduli[2, k, r, :] * shear, common + twice * dy1
+            if energy is not None and k < extra:
+                energy = energy + (xx * dx0 + yy * dy1 + xy * shear)
+            stress[0, k, s, :] = xx
+            stress[1, k, s, :] = xy
+            stress[2, k, s, :] = yy
+        return energy
+
+    def row_before():
+        for q in range(3):
+            for k in range(SIDE):
+                stress[q, k, 0:8, :] = stress[q, k, rows + 8 : rows + 16, :]
+
+    def forces(level, base, acc, where, border=False, final=False):
+        r, s, b = pl.ds(base, 8), pl.ds(base + 8, 8), pl.ds(base + 7, 8)
+        before = {(k - 1) % SIDE for k in where}
+        behind = set() if final else {(k + 1) % SIDE for k in where}
+        plain, moved = ({}, {}), ({}, {})
+        for k in sorted(before | behind | set(where)):
+            xx, xy, yy = stress[0, k, s, :], stress[1, k, s, :], stress[2, k, s, :]
+            xx_b, xy_b, yy_b = stress[0, k, b, :], stress[1, k, b, :], stress[2, k, b, :]
+            dxx, sxy, dxy, syy = xx_b - xx, xy_b + xy, xy_b - xy, yy_b + yy
+            if k in where or k in behind:
+                plain[0][k] = dxx - sxy
+                plain[1][k] = dxy - syy
+            if k in where or k in before:
+                moved[0][k] = dxx + sxy
+                moved[1][k] = dxy + syy
+        for c in range(2):
+            turned = {k: pltpu.roll(x, 1, 1) for k, x in moved[c].items()}
+            returned = {} if final else {k: pltpu.roll(x, 127, 1) for k, x in plain[c].items()}
+            for k in where:
+                old = v[level, c, k, r, :]
+                value = plain[c][k] + jnp.where(first_lane, turned[(k - 1) % SIDE], turned[k])
+                if level:
+                    value = value - old
+                if final:
+                    v[level + 1, c, k, r, :] = value
+                    continue
+                after = jnp.where(last_lane, returned[(k + 1) % SIDE], returned[k]) + moved[c][k]
+                if level:
+                    after = after - vl[c, k, r, :]
+                if border:
+                    value, after = value * sub_mask, after * sub_mask
+                if k == extra:
+                    value, after = value * lane_mask, after * moved_mask
+                elif k == extra - 1:
+                    after = after * edge_mask
+                if k < extra and not border:
+                    acc = (acc[0] + old * value, acc[1] + value * value)
+                v[level + 1, c, k, r, :] = value
+                vl[c, k, r, :] = after
+        return acc
+
+    def vector_done(level, acc):
+        for c in range(2):
+            for k in range(SIDE):
+                v[level + 1, c, k, again, :] = v[level + 1, c, k, 0:8, :]
+                vl[c, k, again, :] = vl[c, k, 0:8, :]
+        moments[2 * level + 1] = acc[0]
+        moments[2 * level + 2] = acc[1]
+
+    def rows_from(t):
+        return pl.multiple_of(8 * t, 8)
+
+    inside = tuple(range(1, planes - 1))
+    outside = tuple(k for k in everywhere if k not in inside)
+
+    def stress_inside(t, carry):
+        stresses(0, rows_from(t), range(planes))
+        return carry
+
+    loop(tiles - 1, stress_inside, 0)
+    acc = loop(tiles - 2, lambda t, acc: forces(0, rows_from(t + 1), acc, inside), (zero, zero))
+
+    pl.semaphore_wait(met.at[0], len(WAYS))
+    for dx, dy in WAYS:
+        pl.semaphore_signal(met.at[1], inc=1, device_id=at(2 * dx, 2 * dy), device_id_type=MESH)
+
+    def arrived(ways):
+        for index in range(len(WAYS)):
+            dx, dy = WAYS[index]
+            if (dx, dy) in ways:
+                @pl.when(has[-dx, -dy])
+                def _(index=index):
+                    for copy in copies(index):
+                        copy.wait_recv()
+
+    def beside_moduli(part):
+        left, right = looked_up(mat_halo[0, part, :]), looked_up(mat_halo[2, part, :])
+        size = part.stop - part.start
+        wide_lane = lax.broadcasted_iota(jnp.int32, (size, 128), 1)
+        for q in range(2):
+            near = jnp.broadcast_to(right[q][:, 0:1], (size, 128))
+            far = jnp.broadcast_to(left[q][:, mat_cols - 1 : mat_cols], (size, 128))
+            compact[q, part, :] = jnp.where(wide_lane < 64, near, far)
+
+    arrived([(0, -1), (0, 1)])
+    for c in range(2):
+        beside = col_halo[c].T
+        for t in range(tiles):
+            v[0, c, extra, 8 * t : 8 * t + 8, :] = jnp.where(inner_lanes, beside[8 * t : 8 * t + 8], 0.0)
+    beside_moduli(slice(0, mat_rows))
+    for t in range(tiles):
+        lam, mu = (
+            jnp.where(inner_lanes, jnp.broadcast_to(compact[q, t : t + 1, :], (8, 128)), 0.0) for q in range(2)
+        )
+        put_moduli((extra, slice(8 * t, 8 * t + 8)), lam, mu)
+
+    def rest_shift(t, carry):
+        r = pl.ds(rows_from(t), 8)
+        for c in range(2):
+            near, far, start = (v[0, c, k, r, :] for k in (planes - 1, extra, 0))
+            for k, value in enumerate(shifted_left([near, far, start])[:-1]):
+                vl[c, planes - 1 + k, r, :] = value
+        return carry
+
+    loop(tiles, rest_shift, 0)
+
+    def stress_outside(t, carry):
+        stresses(0, rows_from(t), (planes - 1, extra))
+        return carry
+
+    loop(tiles - 1, stress_outside, 0)
+    acc = loop(tiles - 2, lambda t, acc: forces(0, rows_from(t + 1), acc, outside), acc)
+
+    arrived([way for way in WAYS if way[0]])
     for c in range(2):
         for k in range(planes):
             part = slice(128 * k, 128 * (k + 1))
             ring = jnp.where(low, row_halo[0, c, :, part], row_halo[1, c, :, part])
             v[0, c, k, halo, :] = jnp.where(inner_subs, ring, 0.0)
-            v[0, c, k, again, :] = load[0, c, 0:8, part]
-        beside = col_halo[c].T
-        for t in range(tiles):
-            value = jnp.where(inner_lanes, beside[8 * t : 8 * t + 8], 0.0)
-            v[0, c, extra, 8 * t : 8 * t + 8, :] = value
-            if t == 0:
-                v[0, c, extra, again, :] = value
         below = jnp.where(left_lanes, corner[0, 1, c], corner[0, 0, c])
         above = jnp.where(left_lanes, corner[1, 1, c], corner[1, 0, c])
         v[0, c, extra, halo, :] = jnp.where(inner_both, jnp.where(low, below, above), 0.0)
-
+        for k in range(SIDE):
+            v[0, c, k, again, :] = v[0, c, k, 0:8, :]
     beyond = widened(mat_halo[1, mat_rows : mat_rows + 16, :])
     for k in range(planes):
         part = slice(128 * k, 128 * (k + 1))
@@ -227,17 +359,7 @@
             for m in beyond
         )
         put_moduli((k, halo), lam, mu)
-    left, right = looked_up(mat_halo[0]), looked_up(mat_halo[2])
-    for q in range(2):
-        near = jnp.broadcast_to(right[q][:, 0:1], (mat_rows + 16, 128))
-        far = jnp.broadcast_to(left[q][:, mat_cols - 1 : mat_cols], (mat_rows + 16, 128))
-        wide_lane = lax.broadcasted_iota(jnp.int32, (mat_rows + 16, 128), 1)
-        compact[q] = jnp.where(wide_lane < 64, near, far)
-    for t in range(tiles):
-        lam, mu = (
-            jnp.where(inner_lanes, jnp.broadcast_to(compact[q, t : t + 1, :], (8, 128)), 0.0) for q in range(2)
-        )
-        put_moduli((extra, slice(8 * t, 8 * t + 8)), lam, mu)
+    beside_moduli(slice(mat_rows, mat_rows + 16))
     lam, mu = (
         jnp.where(
             inner_both,
@@ -251,118 +373,36 @@
         for q in range(2)
     )
     put_moduli((extra, halo), lam, mu)
-
-    def rest_shift(t, carry):
-        r = pl.ds(pl.multiple_of(8 * t, 8), 8)
-        for c in range(2):
-            near, far, start = (v[0, c, k, r, :] for k in (planes - 1, extra, 0))
-            for k, value in enumerate(shifted_left([near, far, start])[:-1]):
-                vl[c, planes - 1 + k, r, :] = value
-        return carry
-
-    loop(tiles, rest_shift, 0)
     for c in range(2):
         for k, value in enumerate(shifted_left([v[0, c, k, halo, :] for k in range(SIDE)])):
             vl[c, k, halo, :] = value
         for k in range(SIDE):
             vl[c, k, again, :] = vl[c, k, 0:8, :]
-
-    beyond_edge = jnp.logical_and(last_lane, jnp.logical_not(has[0, 1]))
-    edge_mask = jnp.where(beyond_edge, 0.0, 1.0)
-    moved_lanes = jnp.logical_or(
-        jnp.logical_or(jnp.logical_and(lane < 3, has[0, 1]), last_lane),
-        jnp.logical_and(jnp.logical_and(lane >= 123, lane < 127), has[0, -1]),
-    )
-    moved_mask = moved_lanes.astype(jnp.float32)
-
-    pl.semaphore_wait(met.at[0], len(WAYS))
-    for dx, dy in WAYS:
-        pl.semaphore_signal(met.at[1], inc=1, device_id=at(2 * dx, 2 * dy), device_id_type=MESH)
-
-    def stresses(level, tally):
-        def body(t, energy):
-            base = pl.multiple_of(8 * t, 8)
-            r, rr = pl.ds(base, 8), pl.ds(base + 1, 8)
-            for k in range(SIDE):
-                d = []
-                for c in range(2):
-                    u = vl[c, k, rr, :] - v[level, c, k, r, :]
-                    w = v[level, c, k, rr, :] - vl[c, k, r, :]
-                    d.append((u + w, u - w))
-                (dx0, dy0), (dx1, dy1) = d
-                volume, shear = dx0 + dy1, dy0 + dx1
-                common = moduli[0, k, r, :] * volume
-                twice = moduli[1, k, r, :]
-                xx, xy, yy = common + twice * dx0, moduli[2, k, r, :] * shear, common + twice * dy1
-                if tally and k < extra:
-                    energy = energy + (xx * dx0 + yy * dy1 + xy * shear)
-                s = pl.ds(base + 8, 8)
-                stress[0, k, s, :] = xx
-                stress[1, k, s, :] = xy
-                stress[2, k, s, :] = yy
-            return energy
-
-        energy = loop(tiles, body, jnp.zeros((8, 128), jnp.float32))
-        tally = False
-        body(tiles, energy)
-        for q in range(3):
-            for k in range(SIDE):
-                stress[q, k, 0:8, :] = stress[q, k, rows + 8 : rows + 16, :]
-        return energy
-
-    def forces(level, base, acc, border, final):
-        r, s, b = pl.ds(base, 8), pl.ds(base + 8, 8), pl.ds(base + 7, 8)
-        plain, moved = ([], []), ([], [])
-        for k in range(SIDE):
-            xx, xy, yy = stress[0, k, s, :], stress[1, k, s, :], stress[2, k, s, :]
-            xx_b, xy_b, yy_b = stress[0, k, b, :], stress[1, k, b, :], stress[2, k, b, :]
-            dxx, sxy, dxy, syy = xx_b - xx, xy_b + xy, xy_b - xy, yy_b + yy
-            plain[0].append(dxx - sxy)
-            moved[0].append(dxx + sxy)
-            plain[1].append(dxy - syy)
-            moved[1].append(dxy + syy)
-        for c in range(2):
-            here = shifted_right(moved[c])
-            there = None if final else shifted_left(plain[c])
-            for k in range(planes if final else SIDE):
-                old = v[level, c, k, r, :]
-                value = plain[c][k] + here[k]
-                if level:
-                    value = value - old
-                if final:
-                    v[level + 1, c, k, r, :] = value
-                    continue
-                after = there[k] + moved[c][k]
-                if level:
-                    after = after - vl[c, k, r, :]
-                if border:
-                    value, after = value * sub_mask, after * sub_mask
-                if k == extra:
-                    value, after = value * lane_mask, after * moved_mask
-                elif k == extra - 1:
-                    after = after * edge_mask
-                if k < extra and not border:
-                    acc = (acc[0] + old * value, acc[1] + value * value)
-                v[level + 1, c, k, r, :] = value
-                vl[c, k, r, :] = after
-        return acc
-
-    zero = jnp.zeros((8, 128), jnp.float32)
-    for level in range(LEVELS - 1):
-        stresses(level, False)
+    stresses(0, rows - 8, everywhere)
+    stresses(0, rows, everywhere)
+    row_before()
+    acc = forces(0, 0, acc, everywhere)
+    acc = forces(0, rows - 8, acc, everywhere)
+    forces(0, rows, None, everywhere, border=True)
+    vector_done(0, acc)
+
+    for level in range(1, LEVELS - 1):
+        def stress_step(t, carry, level=level):
+            stresses(level, rows_from(t), everywhere)
+            return carry
+
+        loop(tiles + 1, stress_step, 0)
+        row_before()
         acc = loop(
-            tiles,
-            lambda t, acc, level=level: forces(level, pl.multiple_of(8 * t, 8), acc, False, False),
-            (zero, zero),
+            tiles, lambda t, acc, level=level: forces(level, rows_from(t), acc, everywhere), (zero, zero)
         )
-        forces(level, rows, None, True, False)
-        for c in range(2):
-            for k in range(SIDE):
-                v[level + 1, c, k, again, :] = v[level + 1, c, k, 0:8, :]
-                vl[c, k, again, :] = vl[c, k, 0:8, :]
-        moments[2 * level + 1] = acc[0]
-        moments[2 * level + 2] = acc[1]
-    moments[2 * LEVELS - 1] = stresses(LEVELS - 1, True) + DIAG * moments[2 * LEVELS - 2]
+        forces(level, rows, None, everywhere, border=True)
+        vector_done(level, acc)
+    last = LEVELS - 1
+    energy = loop(tiles, lambda t, energy: stresses(last, rows_from(t), everywhere, energy), zero)
+    stresses(last, rows, everywhere)
+    row_before()
+    moments[2 * LEVELS - 1] = energy + DIAG * moments[2 * LEVELS - 2]
 
     partial = jnp.sum(moments[0 : 2 * LEVELS], axis=1)
     partial = jnp.sum(partial, axis=1, keepdims=True)
@@ -384,7 +424,7 @@
     )
 
     def final_forces(t, carry):
-        forces(LEVELS - 1, pl.multiple_of(8 * t, 8), None, False, True)
+        forces(last, rows_from(t), None, range(planes), final=True)
         return carry
 
     loop(tiles, final_forces, 0)

time: 23.4 us -> 23 us (0.983)
  Pallas kernels: 22.6 us -> 22.3 us
    pallas_call x1, Pallas kernels: 21.6 us -> 21.2 us  [on_device(): pl.pallas_call(functools.partial(kernel, nx, ny), out_shape=[jax.ShapeDty...]
where the time goes in v4:
time: 23 us; the launch traced here: 22.9 us
  Pallas kernels  22.3 us (97%)
  between operations  0.64 us (3%)
    pallas_call x1, Pallas kernels, on_device(): pl.pallas_call(functools.partial(kernel, nx, ny), out_shape=[jax.ShapeDty...  21.2 us
    pallas_call x1, Pallas kernels, on_device(): pl.pallas_call(combine, out_shape=[jax.ShapeDtypeStruct(load.shape, f32)]...  1.07 us

profile of v4, /device:TPU:1, one launch (start us, length us, event | category | flops | bytes accessed | tf_op | source)
XLA Modules:
  0.0 22.9 jit_solution(2681612011564698153)
XLA Ops:
  0.6 21.2 %shard_map.50 = (f32[5,2,5,144,128]{4,3,2,1,0:T(8,128)S(1)}, f32[9,8,128]{2,1,0:T(8,128)S(1)}) custom-call(f32[1,2,128,512]{3,2,1,0:T(8,128)} %load_in.1, s32[1,16,64]{2,1,0:T(8,128)} %material_in.1, f32[2,8]{1,0:T(2,128)} %table_in.1), custom_call_target="tpu_custom_call" | custom-call | tf_op jit(solution)/shard_map/pallas_call | solution.py:515
  21.9 1.1 %shard_map.51 = (f32[1,2,128,512]{3,2,1,0:T(8,128)}, f32[1,2,128,512]{3,2,1,0:T(8,128)}) custom-call(f32[5,2,5,144,128]{4,3,2,1,0:T(8,128)S(1)} %get-tuple-element.4.v, f32[9,8,128]{2,1,0:T(8,128)S(1)} %get-tuple-element.5.factors), custom_call_target="tpu_custom_call" | custom-call | tf_op jit(solution)/shard_map/pallas_call | solution.py:550
